TPU v7x, 32 devices: a whole 2x2x4 slice. The times are simulated.
32 devices in a mesh: lat: 4 (over x, core), lon: 8 (over z, y).
Axes of the slice: x: 2, y: 2, z: 4, core: 2. Of those that a mesh axis runs over, the one named last changes fastest.
Arguments:
- background: bfloat16 [16, 256, 2560], P('lat', 'lon'), may hold values from -6 to 6
- band_cols: int32 [16], P('lat'), may hold values from 20 to 256, as said below
- obs_col: int32 [16, 512], P('lat', 'lon'), may hold values from 0 to 255, as said below
- obs_lev: int32 [16, 512], P('lat', 'lon'), may hold values from 0 to 39
- obs_mask: int32 [16, 512], P('lat', 'lon'), may hold values from 0 to 1, as said below
- innov: float32 [16, 512], P('lat', 'lon'), may hold values from -9 to 9
- obs_var: float32 [16, 512], P('lat', 'lon'), may hold values from 0.25 to 2.5
Outputs:
- analysis: bfloat16 [16, 256, 2560], P('lat', 'lon')
Inputs may be any that keep to these rules, and one draw needn't show every extreme that they name: Band 0 has 20 columns, band 16 // 2 has 160 columns and the last band 256; columns from band_cols on are padding. `obs_col`: slot i of a band lies in the columns from i // 64 * 32 to that plus 32 - 1. An observation in use lies below its band's band_cols. No column holds more than 4 observations in use, and some column of every band holds exactly 4. `obs_mask`: 1 marks an observation in use.
All inputs are finite; a program needn't handle non-finite values.
Results may differ from a plain program's by a relative error of at most 0.0061.
Values may be sent and summed in bfloat16 or wider, within the bound.
A program may use at most 128 MiB of HBM per device.

v0:
```python
import functools

import jax
import jax.numpy as jnp
from jax import lax
from jax.experimental import pallas as pl
from jax.experimental.pallas import tpu as pltpu
from jax.sharding import PartitionSpec as P

K = 64
LEV = 40
RADIUS = 8
ITERS = 4
GROUP = 4
OC = 4
END_SLOTS = 32
FAR = 1 << 20
LANES = 128
F32 = jnp.float32
BF16 = jnp.bfloat16
MESH = pl.DeviceIdType.MESH


def taper_weights(radius):
    half_width = radius / 2.0
    tapering = []
    for offset in range(radius):
        distance = offset / half_width
        if distance <= 1.0:
            weight = (
                ((-0.25 * distance + 0.5) * distance + 0.625) * distance**3
                - 5.0 / 3.0 * distance**2
                + 1.0
            )
        else:
            weight = (
                (((distance / 12.0 - 0.5) * distance + 0.625) * distance + 5.0 / 3.0) * distance**2
                - 5.0 * distance
                + 4.0
                - 2.0 / (3.0 * distance)
            )
        tapering.append(weight)
    return tapering


def dot(left, right):
    return jnp.dot(left, right, preferred_element_type=F32)


def iota(shape, dim):
    return lax.broadcasted_iota(jnp.int32, shape, dim)


def exchange_kernel(
    lats,
    lons,
    x_ref,
    col_ref,
    lev_ref,
    mask_ref,
    innov_ref,
    var_ref,
    cols_ref,
    own_ref,
    side_ref,
    shift_ref,
    ends_buf,
    near_buf,
    tail_buf,
    lat_buf,
    lon_buf,
    near_send,
    near_recv,
    head_send,
    head_recv,
    tail_send,
    tail_recv,
    lat_send,
    lat_recv,
    lon_send,
    lon_recv,
):
    lat, lon = lax.axis_index("lat"), lax.axis_index("lon")
    barrier = pltpu.get_barrier_semaphore()
    near_buf[...] = jnp.zeros_like(near_buf)
    tail_buf[...] = jnp.zeros_like(tail_buf)

    def greet_lon(step, carry):
        pl.semaphore_signal(
            barrier, inc=1, device_id=(lat, lax.rem(lon + step, lons)), device_id_type=MESH
        )
        return carry

    def greet_lat(step, carry):
        pl.semaphore_signal(
            barrier, inc=1, device_id=(lax.rem(lat + step, lats), lon), device_id_type=MESH
        )
        return carry

    lax.fori_loop(1, lons, greet_lon, 0)
    lax.fori_loop(1, lats, greet_lat, 0)

    bands, columns, width = x_ref.shape
    obs = col_ref.shape[1]
    half = obs // 2
    pairs = width // LANES
    reach = RADIUS - 1
    ends = END_SLOTS
    first = lon * columns
    local_int = col_ref[...] - first
    local = local_int.astype(F32)
    mask = mask_ref[...].astype(F32)
    scale = jnp.sqrt(mask / var_ref[...])
    params = jnp.concatenate([local, lev_ref[...].astype(F32), scale, innov_ref[...]], axis=0)
    params = jnp.concatenate([params, jnp.zeros((LANES - 4 * bands, obs), F32)], axis=0)
    params = jnp.concatenate([params, jnp.zeros((LANES, LANES - obs), F32)], axis=1)
    upright = jnp.transpose(params)[:obs]
    col_ids = iota((obs, columns), 1)
    earlier = iota((obs, obs), 0) < iota((obs, obs), 1)
    slot_ids = iota((ends, obs), 0)
    def stacked(kind):
        return jnp.concatenate(
            [upright[:, kind * bands + b : kind * bands + b + 1] for b in range(bands)], axis=0
        )

    levels = stacked(1).astype(jnp.int32)
    scales = stacked(2)
    gathered = []
    for b in range(bands):
        col = upright[:, b : b + 1]
        onehot = jnp.where(col_ids == col.astype(jnp.int32), 1.0, 0.0).astype(BF16)
        pair = lax.shift_right_logical(levels[b * obs : (b + 1) * obs], 1)
        found = jnp.zeros((obs, LANES), F32)
        for p in range(pairs):
            got = dot(onehot, x_ref[b, :, p * LANES : (p + 1) * LANES])
            found = jnp.where(pair == p, got, found)
        gathered.append(found)
    found = jnp.concatenate(gathered, axis=0)
    picked = jnp.where((levels & 1) == 1, found[:, K:], found[:, :K])
    anomaly = picked - jnp.mean(picked, axis=1, keepdims=True)
    departs = (scales * (anomaly - stacked(3))).astype(BF16)
    wide = departs.astype(F32)
    centre = jnp.mean(wide, axis=1, keepdims=True)
    spread = wide - centre
    centre_sum = centre * centre
    spread_sum = spread * spread
    for b in range(bands):
        col = upright[:, b : b + 1]
        depart_scale = upright[:, 2 * bands + b : 2 * bands + b + 1]
        narrow = departs[b * obs : (b + 1) * obs]
        depart = wide[b * obs : (b + 1) * obs]
        packed = jnp.concatenate([depart[:half], depart[half:]], axis=1)
        own_ref[b * half : (b + 1) * half, :] = packed.astype(BF16)
        row = local_int[b : b + 1]
        used = mask[b : b + 1] > 0.0
        same = (col == local[b : b + 1]) & (depart_scale > 0.0) & earlier
        rank = jnp.sum(jnp.where(same, 1.0, 0.0), axis=0, keepdims=True).astype(jnp.int32)
        bases = (row, row - (columns - reach), row + first - (cols_ref[b] - reach))
        marks = []
        for base in bases:
            fits = used & (base >= 0) & (base < reach)
            slot = jnp.where(fits, base * OC + rank, -1)
            marks.append(jnp.where(slot_ids == slot, 1.0, 0.0))
        compact = dot(jnp.concatenate(marks, axis=0).astype(BF16), narrow)
        for kind in range(3):
            low = kind * ends
            packed = jnp.concatenate(
                [compact[low : low + ends // 2], compact[low + ends // 2 : low + ends]], axis=1
            )
            ends_buf[kind, b * ends // 2 : (b + 1) * ends // 2, :] = packed.astype(BF16)
    numerator = jnp.sum(centre_sum, axis=0, keepdims=True)
    spread_row = jnp.sum(spread_sum, axis=0, keepdims=True)
    mask_row = jnp.sum(mask, axis=0, keepdims=True)
    denominator = jnp.sum(spread_row / (K - 1), axis=1, keepdims=True) + jnp.sum(
        mask_row, axis=1, keepdims=True
    )
    stat_lane = iota((8, LANES), 1)
    lat_buf[lat] = jnp.where(stat_lane == 0, numerator, denominator)

    pl.semaphore_wait(barrier, lons + lats - 2)

    def lat_copy(slot, step, other):
        return pltpu.make_async_remote_copy(
            src_ref=lat_buf.at[slot],
            dst_ref=lat_buf.at[slot],
            send_sem=lat_send.at[step],
            recv_sem=lat_recv.at[slot],
            device_id=(other, lon),
            device_id_type=MESH,
        )

    def lon_copy(slot, step, other):
        return pltpu.make_async_remote_copy(
            src_ref=lon_buf.at[slot],
            dst_ref=lon_buf.at[slot],
            send_sem=lon_send.at[step],
            recv_sem=lon_recv.at[slot],
            device_id=(lat, other),
            device_id_type=MESH,
        )

    def near_copy(kind, slot, other):
        return pltpu.make_async_remote_copy(
            src_ref=ends_buf.at[kind],
            dst_ref=near_buf.at[slot],
            send_sem=near_send.at[slot],
            recv_sem=near_recv.at[slot],
            device_id=(lat, other),
            device_id_type=MESH,
        )

    def head_copy(other):
        return pltpu.make_async_remote_copy(
            src_ref=ends_buf.at[0],
            dst_ref=near_buf.at[2],
            send_sem=head_send.at[other],
            recv_sem=head_recv,
            device_id=(lat, other),
            device_id_type=MESH,
        )

    def tail_copy(slot):
        return pltpu.make_async_remote_copy(
            src_ref=ends_buf.at[2],
            dst_ref=tail_buf.at[slot],
            send_sem=tail_send,
            recv_sem=tail_recv.at[slot],
            device_id=(lat, 0),
            device_id_type=MESH,
        )

    for step in range(1, lats):
        lat_copy(lat, step, lax.rem(lat + step, lats)).start()

    @pl.when(lon > 0)
    def _():
        tail_copy(lon).start()
        near_copy(0, 1, lon - 1).start()

    @pl.when(lon == 0)
    def _():
        def send(other, carry):
            head_copy(other).start()
            return carry

        lax.fori_loop(1, lons, send, 0)

    @pl.when(lon < lons - 1)
    def _():
        near_copy(1, 0, lon + 1).start()

    for step in range(1, lats):
        source = lax.rem(lat + lats - step, lats)
        lat_copy(source, step, source).wait_recv()
    lon_buf[lon] = jnp.sum(lat_buf[...], axis=0)

    def send_lon(step, carry):
        lon_copy(lon, step, lax.rem(lon + step, lons)).start()
        return carry

    lax.fori_loop(1, lons, send_lon, 0)
    for step in range(1, lats):
        lat_copy(lat, step, lax.rem(lat + step, lats)).wait_send()

    @pl.when(lon > 0)
    def _():
        near_copy(1, 0, lon - 1).wait_recv()
        head_copy(lon).wait_recv()
        tail_copy(lon).wait_send()
        near_copy(0, 1, lon - 1).wait_send()

    @pl.when(lon == 0)
    def _():
        def take(other, carry):
            head_copy(other).wait_send()
            tail_copy(other).wait_recv()
            return carry

        lax.fori_loop(1, lons, take, 0)

    @pl.when(lon < lons - 1)
    def _():
        near_copy(0, 1, lon + 1).wait_recv()
        near_copy(1, 0, lon + 1).wait_send()

    side_ref[0] = (
        near_buf[0].astype(F32) + jnp.sum(tail_buf[...].astype(F32), axis=0)
    ).astype(BF16)
    side_ref[1] = near_buf[1]
    side_ref[2] = near_buf[2]

    def take_lon(step, carry):
        lon_copy(lon, step, lax.rem(lon + step, lons)).wait_send()
        source = lax.rem(lon + lons - step, lons)
        lon_copy(source, step, source).wait_recv()
        return carry

    lax.fori_loop(1, lons, take_lon, 0)
    stats = jnp.sum(lon_buf[...], axis=0)
    inflation = (stats[:, 0:1] + 1e-06) / stats[:, 1:2]
    shift_ref[...] = jnp.broadcast_to((K - 1) / inflation, (8, LANES))


def analysis_kernel(
    x_ref, own_ref, side_ref, shift_ref, col_ref, cols_ref, out_ref, xs, ys, w_s, st_s, rhs_s, gs
):
    lon = lax.axis_index("lon")
    bands, columns, width = x_ref.shape
    half = own_ref.shape[0] // bands
    quarter = side_ref.shape[1] // bands
    held = LANES
    obs = 2 * held
    sides = half + 3 * quarter
    pairs = width // LANES
    groups = columns // GROUP
    span = GROUP * K
    tapering = taper_weights(RADIUS)
    shift = shift_ref[0:1, 0:1]
    low = iota((K, LANES), 1) < K
    low_f = jnp.where(low, 1.0, 0.0)
    low_b = low_f.astype(BF16)
    high_b = (1.0 - low_f).astype(BF16)
    zero_b = jnp.zeros((K, LANES), BF16)
    rows_x = xs.shape[0] // columns
    low_x = iota((rows_x, LANES), 1) < K
    eye = jnp.where(iota((K, span), 0) == iota((K, span), 1) % K, 1.0, 0.0)

    def block_diag(mat):
        left, right = mat[:, :LANES], mat[:, LANES:]
        return jnp.concatenate(
            [
                jnp.concatenate([left * low_b, zero_b], axis=1),
                jnp.concatenate([left * high_b, zero_b], axis=1),
                jnp.concatenate([zero_b, right * low_b], axis=1),
                jnp.concatenate([zero_b, right * high_b], axis=1),
            ],
            axis=0,
        )

    ones_bd = block_diag(jnp.ones((K, span), BF16))

    def one_band(b, carry):
        count = cols_ref[b]
        for p in range(pairs):
            strip = x_ref[b, :, p * LANES : (p + 1) * LANES].astype(F32)
            xs[pl.ds(p, columns, stride=rows_x), :] = strip
        start = pl.multiple_of(b * half, half)
        side = pl.multiple_of(b * quarter, quarter)
        block = jnp.concatenate(
            [own_ref[pl.ds(start, half), :]]
            + [side_ref[kind, pl.ds(side, quarter), :] for kind in range(3)]
            + [jnp.zeros((held - sides, LANES), BF16)],
            axis=0,
        ).astype(F32)
        turned = jnp.transpose(block)
        depart_t = jnp.concatenate([turned[:K], turned[K:]], axis=1)
        centre = jnp.mean(depart_t, axis=0, keepdims=True)
        st_s[...] = depart_t - centre
        rolled = pltpu.roll(block, K, 1)
        low_h = iota((held, LANES), 1) < K
        rhs = jnp.concatenate(
            [jnp.where(low_h, block, rolled), jnp.where(low_h, rolled, block)], axis=0
        )
        rhs_s[...] = (rhs - jnp.mean(rhs, axis=1, keepdims=True)).astype(BF16)
        col = col_ref[pl.ds(b, 1), :] - lon * columns
        col = jnp.concatenate([col, jnp.zeros((1, held - 2 * half), jnp.int32)], axis=1)
        col = jnp.concatenate([col, jnp.roll(col, -half, axis=1)], axis=1)
        place = iota((1, obs), 1)
        spot = place % held
        slot = spot - half + (place // held) * quarter
        where_left = slot // OC - (RADIUS - 1)
        where_right = (slot - quarter) // OC + columns
        where_head = (slot - 2 * quarter) // OC + count - lon * columns
        source = jnp.where(
            spot < half,
            col,
            jnp.where(
                spot < half + quarter,
                where_left,
                jnp.where(
                    spot < half + 2 * quarter,
                    where_right,
                    jnp.where(spot < sides, where_head, FAR),
                ),
            ),
        )
        limit = jnp.where(spot < half, count, FAR)
        away = source - iota((columns, obs), 0)
        away = jnp.where(2 * away > limit, away - count, away)
        away = jnp.where(2 * away < -limit, away + count, away)
        away = jnp.abs(away)
        weight = jnp.zeros((columns, obs), F32)
        for t in range(RADIUS):
            weight = jnp.where(away == t, tapering[t], weight)
        w_s[...] = weight
        mean_rows = dot((weight * -centre).astype(BF16), rhs_s[...])
        squares = []
        for g in range(groups):
            parts = []
            for c in range(g * GROUP, (g + 1) * GROUP):
                weighted = (st_s[...] * w_s[c : c + 1, :]).astype(BF16)
                parts.append(dot(weighted, rhs_s[...]))
            cat = jnp.concatenate(
                [jnp.where(low, parts[0], parts[1]), jnp.where(low, parts[2], parts[3])], axis=1
            )
            gs[g] = cat
            system = cat + shift * eye
            squares.append(jnp.sum(system * system, axis=0, keepdims=True))
        squares = jnp.concatenate(squares, axis=0)
        coarse = squares.astype(BF16)
        fine = (squares - coarse.astype(F32)).astype(BF16)
        sums = dot(jnp.concatenate([coarse, fine], axis=0), ones_bd)
        frob = jnp.sqrt(sums[:groups] + sums[groups:])
        inv_frob = 1.0 / frob
        scaling = jnp.sqrt((K - 1.0) * inv_frob)
        beta_all = 1.0 - shift * inv_frob
        batch = min(8, groups)
        for first in range(0, groups, batch):
            ids = range(first, first + batch)
            beta = [beta_all[g : g + 1] for g in ids]
            dev = [gs[g] * -inv_frob[g : g + 1] for g in ids]
            zeta = [1.0 + 0.5 * be for be in beta]
            root = [0.5 * d for d in dev]
            for it in range(ITERS):
                narrow = [d.astype(BF16) for d in dev]
                fixed = [block_diag(n) for n in narrow]
                if it == 0:
                    square = [dot(n, f) for n, f in zip(narrow, fixed)]
                elif it + 1 < ITERS:
                    both = [
                        dot(jnp.concatenate([n, r.astype(BF16)], axis=0), f)
                        for n, r, f in zip(narrow, root, fixed)
                    ]
                    square = [x[:K] for x in both]
                    prod = [x[K:] for x in both]
                else:
                    prod = [dot(r.astype(BF16), f) for r, f in zip(root, fixed)]
                if it > 0:
                    root = [
                        (1.0 + 0.5 * be) * r + (0.5 * ze) * d + 0.5 * x
                        for be, r, ze, d, x in zip(beta, root, zeta, dev, prod)
                    ]
                    zeta = [ze * (1.0 + 0.5 * be) for ze, be in zip(zeta, beta)]
                if it + 1 < ITERS:
                    square = [2.0 * be * d + s for be, d, s in zip(beta, dev, square)]
                    cube = [dot(s.astype(BF16), f) for s, f in zip(square, fixed)]
                    dev = [
                        (0.75 + 0.25 * be) * s + (0.25 * be * be) * d + 0.25 * c
                        for be, s, d, c in zip(beta, square, dev, cube)
                    ]
                    beta = [be * be * (0.75 + 0.25 * be) for be in beta]
            full = [ze * eye + r for ze, r in zip(zeta, root)]
            mean_row = []
            for g in ids:
                c0 = g * GROUP
                m = [mean_rows[c : c + 1] for c in range(c0, c0 + GROUP)]
                mean_row.append(
                    jnp.concatenate(
                        [jnp.where(low[:1], m[0], m[1]), jnp.where(low[:1], m[2], m[3])], axis=1
                    )
                )
            half_step = [
                ze * m
                + dot(
                    jnp.broadcast_to(m, (8, span)).astype(BF16), block_diag(r.astype(BF16))
                )[:1]
                for ze, m, r in zip(zeta, mean_row, root)
            ]
            shifted = [
                dot((f * h).astype(BF16), ones_bd) for f, h in zip(full, half_step)
            ]
            mix = []
            for f, ze, sh, g in zip(full, zeta, shifted, ids):
                scale = scaling[g : g + 1]
                mix.append(
                    (
                        scale * f
                        + (1.0 - scale * ze) * (1.0 / K)
                        + sh * inv_frob[g : g + 1]
                    ).astype(BF16)
                )
            applied = []
            for g, mx in zip(ids, mix):
                c0 = g * GROUP
                sides_in = []
                for c in (c0, c0 + 2):
                    here = xs[c * rows_x : (c + 1) * rows_x, :]
                    there = xs[(c + 1) * rows_x : (c + 2) * rows_x, :]
                    even = jnp.where(low_x, here, pltpu.roll(there, K, 1))
                    odd = jnp.where(low_x, pltpu.roll(here, K, 1), there)
                    sides_in.append(jnp.concatenate([even, odd], axis=0).astype(BF16))
                applied.append(dot(jnp.concatenate(sides_in, axis=1), block_diag(mx)))
            for g, result in zip(ids, applied):
                c0 = g * GROUP
                for side, c in enumerate((c0, c0 + 2)):
                    got = result[:, side * LANES : (side + 1) * LANES]
                    even, odd = got[:rows_x], got[rows_x:]
                    ys[c * rows_x : (c + 1) * rows_x, :] = jnp.where(low_x, even, pltpu.roll(odd, K, 1))
                    ys[(c + 1) * rows_x : (c + 2) * rows_x, :] = jnp.where(low_x, pltpu.roll(even, K, 1), odd)
        keep = lon * columns + iota((columns, LANES), 0) < count
        for p in range(pairs):
            out_ref[b, :, p * LANES : (p + 1) * LANES] = jnp.where(
                keep, ys[pl.ds(p, columns, stride=rows_x), :], 0.0
            ).astype(BF16)
        return carry

    lax.fori_loop(0, bands, one_band, 0)


def per_device(lats, lons, background, band_cols, obs_col, obs_lev, obs_mask, innov, obs_var):
    bands, columns, width = background.shape
    obs = obs_col.shape[1]
    pairs = width // LANES
    vmem = pl.BlockSpec(memory_space=pltpu.VMEM)
    smem = pl.BlockSpec(memory_space=pltpu.SMEM)
    dma = pltpu.SemaphoreType.DMA
    end_rows = bands * END_SLOTS // 2
    padded_pairs = -(-pairs // 8) * 8
    own, side, shift = pl.pallas_call(
        functools.partial(exchange_kernel, lats, lons),
        out_shape=(
            jax.ShapeDtypeStruct((bands * obs // 2, LANES), BF16),
            jax.ShapeDtypeStruct((3, end_rows, LANES), BF16),
            jax.ShapeDtypeStruct((8, LANES), F32),
        ),
        in_specs=[vmem] * 6 + [smem],
        out_specs=(vmem, vmem, vmem),
        scratch_shapes=[
            pltpu.VMEM((3, end_rows, LANES), BF16),
            pltpu.VMEM((3, end_rows, LANES), BF16),
            pltpu.VMEM((lons, end_rows, LANES), BF16),
            pltpu.VMEM((lats, 8, LANES), F32),
            pltpu.VMEM((lons, 8, LANES), F32),
            dma((2,)),
            dma((2,)),
            dma((lons,)),
            dma,
            dma,
            dma((lons,)),
            dma((lats,)),
            dma((lats,)),
            dma((lons,)),
            dma((lons,)),
        ],
        compiler_params=pltpu.CompilerParams(collective_id=0, has_side_effects=True),
        name="exchange",
    )(background, obs_col, obs_lev, obs_mask, innov, obs_var, band_cols)
    return pl.pallas_call(
        analysis_kernel,
        out_shape=jax.ShapeDtypeStruct(background.shape, BF16),
        in_specs=[vmem] * 5 + [smem],
        out_specs=vmem,
        scratch_shapes=[
            pltpu.VMEM((columns * padded_pairs, LANES), F32),
            pltpu.VMEM((columns * padded_pairs, LANES), F32),
            pltpu.VMEM((columns, 2 * LANES), F32),
            pltpu.VMEM((K, 2 * LANES), F32),
            pltpu.VMEM((2 * LANES, LANES), BF16),
            pltpu.VMEM((columns // GROUP, K, GROUP * K), F32),
        ],
        name="analysis",
    )(background, own, side, shift, obs_col, band_cols)


def solution(mesh):
    placed = (P("lat", "lon", None), P("lat")) + (P("lat", "lon"),) * 5
    return jax.shard_map(
        functools.partial(per_device, mesh.shape["lat"], mesh.shape["lon"]),
        mesh=mesh,
        in_specs=placed,
        out_specs=P("lat", "lon", None),
        check_vma=False,
    )
```

profile of v0, /device:TPU:0, one launch (start us, length us, event | category | flops | bytes accessed | tf_op | source)
XLA Modules:
  0.0 29.3 jit_solution(1694672961574327136)
XLA Ops:
  0.0 15.0 %exchange.1 = (bf16[128,128]{1,0:T(8,128)(2,1)}, bf16[3,64,128]{2,1,0:T(8,128)(2,1)}, f32[8,128]{1,0:T(8,128)}) custom-call(bf16[4,32,2560]{2,1,0:T(8,128)(2,1)} %x_ref.3, s32[4,64]{1,0:T(4,128)} %col_ref.3, s32[4,64]{1,0:T(4,128)} %lev_ref.1, s32[4,64]{1,0:T(4,128)} %mask_ref.1, f32[4,64]{1,0:T(4,128)} %innov_ref.1, f32[4,64]{1,0:T(4,128)} %var_ref.1, ...), custom_call_target="tpu_custom_call" | custom-call | tf_op jit(solution)/shard_map/exchange/pallas_call | solution.py:519
  15.0 14.3 %analysis.1 = bf16[4,32,2560]{2,1,0:T(8,128)(2,1)} custom-call(bf16[4,32,2560]{2,1,0:T(8,128)(2,1)} %x_ref.3, bf16[128,128]{1,0:T(8,128)(2,1)} %get-tuple-element.8.own_ref, bf16[3,64,128]{2,1,0:T(8,128)(2,1)} %get-tuple-element.9.side_ref, f32[8,128]{1,0:T(8,128)} %get-tuple-element.10.shift_ref, s32[4,64]{1,0:T(4,128)} %col_ref.3, s32[4]{0:T(128)} %cols_ref.3), custom_call_target="tpu_custom_call" | custom-call | tf_op jit(solution)/shard_map/analysis/pallas_call | solution.py:548
where the time goes:
time: 29.5 us; the launch traced here: 29.3 us
  Pallas kernels  29.3 us (99%)
    pallas_call x1, Pallas kernels, per_device(): pl.pallas_call(functools.partial(exchange_kernel, lats, lons), out_shape=...  15 us
    pallas_call x1, Pallas kernels, per_device(): pl.pallas_call(analysis_kernel, out_shape=jax.ShapeDtypeStruct(background...  14.3 us

commit v1 on v0

v1 whole, which is shorter than its diff:
```python
import functools

import jax
import jax.numpy as jnp
from jax import lax
from jax.experimental import pallas as pl
from jax.experimental.pallas import tpu as pltpu
from jax.sharding import PartitionSpec as P

K = 64
RADIUS = 8
GROUP = 4
OC = 4
END_SLOTS = 32
FAR = 1 << 20
LANES = 128
PAIR = 2
SPAN = GROUP * K
F32 = jnp.float32
BF16 = jnp.bfloat16
MESH = pl.DeviceIdType.MESH


def taper_weights(radius):
    half_width = radius / 2.0
    tapering = []
    for offset in range(radius):
        distance = offset / half_width
        if distance <= 1.0:
            weight = (
                ((-0.25 * distance + 0.5) * distance + 0.625) * distance**3
                - 5.0 / 3.0 * distance**2
                + 1.0
            )
        else:
            weight = (
                (((distance / 12.0 - 0.5) * distance + 0.625) * distance + 5.0 / 3.0) * distance**2
                - 5.0 * distance
                + 4.0
                - 2.0 / (3.0 * distance)
            )
        tapering.append(weight)
    return tapering


def dot(left, right):
    return jnp.dot(left, right, preferred_element_type=F32)


def iota(shape, dim):
    return lax.broadcasted_iota(jnp.int32, shape, dim)


def exchange_kernel(
    lats,
    lons,
    x_hbm,
    col_hbm,
    lev_hbm,
    mask_hbm,
    innov_hbm,
    var_hbm,
    cols_hbm,
    own_ref,
    side_ref,
    info_ref,
    w_ref,
    xl_ref,
    x_v,
    col_ref,
    lev_ref,
    mask_ref,
    innov_ref,
    var_ref,
    cols_ref,
    xs,
    ends_buf,
    near_buf,
    tail_buf,
    stat_buf,
    x_sem,
    in_sem,
    near_send,
    near_recv,
    head_send,
    head_recv,
    tail_send,
    tail_recv,
    stat_send,
    stat_recv,
):
    lat, lon = lax.axis_index("lat"), lax.axis_index("lon")
    bands, columns, width = x_v.shape
    obs = col_ref.shape[1]
    devices = lats * lons
    me = lat * lons + lon
    smalls = (
        (col_hbm, col_ref),
        (lev_hbm, lev_ref),
        (mask_hbm, mask_ref),
        (innov_hbm, innov_ref),
        (var_hbm, var_ref),
        (cols_hbm, cols_ref),
    )
    loads = [
        pltpu.make_async_copy(source, target, in_sem.at[i])
        for i, (source, target) in enumerate(smalls)
    ]
    x_loads = [pltpu.make_async_copy(x_hbm.at[b], x_v.at[b], x_sem.at[b]) for b in range(bands)]
    for load in loads + x_loads:
        load.start()
    barrier = pltpu.get_barrier_semaphore()
    near_buf[...] = jnp.zeros_like(near_buf)
    tail_buf[...] = jnp.zeros_like(tail_buf)

    def peer(step):
        other = lax.rem(me + step, devices)
        return lax.div(other, lons), lax.rem(other, lons)

    def greet(step, carry):
        pl.semaphore_signal(barrier, inc=1, device_id=peer(step), device_id_type=MESH)
        return carry

    lax.fori_loop(1, devices, greet, 0)

    pairs = width // LANES
    reach = RADIUS - 1
    ends = END_SLOTS
    first = lon * columns
    for load in loads:
        load.wait()
    local_int = col_ref[...] - first
    local = local_int.astype(F32)
    mask = mask_ref[...].astype(F32)
    scale = jnp.sqrt(mask / var_ref[...])
    params = jnp.concatenate([local, lev_ref[...].astype(F32), scale, innov_ref[...]], axis=0)
    params = jnp.concatenate([params, jnp.zeros((LANES - 4 * bands, obs), F32)], axis=0)
    params = jnp.concatenate([params, jnp.zeros((LANES, LANES - obs), F32)], axis=1)
    upright = jnp.transpose(params)[:obs]
    col_ids = iota((obs, columns), 1)
    earlier = iota((obs, obs), 0) < iota((obs, obs), 1)
    slot_ids = iota((ends, obs), 0)

    def stacked(kind):
        return jnp.concatenate(
            [upright[:, kind * bands + b : kind * bands + b + 1] for b in range(bands)], axis=0
        )

    marks = []
    for b in range(bands):
        col = upright[:, b : b + 1]
        depart_scale = upright[:, 2 * bands + b : 2 * bands + b + 1]
        row = local_int[b : b + 1]
        used = mask[b : b + 1] > 0.0
        same = (col == local[b : b + 1]) & (depart_scale > 0.0) & earlier
        rank = jnp.sum(jnp.where(same, 1.0, 0.0), axis=0, keepdims=True).astype(jnp.int32)
        bases = (row, row - (columns - reach), row + first - (cols_ref[b] - reach))
        mark = []
        for base in bases:
            fits = used & (base >= 0) & (base < reach)
            slot = jnp.where(fits, base * OC + rank, -1)
            mark.append(jnp.where(slot_ids == slot, 1.0, 0.0))
        marks.append(jnp.concatenate(mark, axis=0).astype(BF16))

    levels = stacked(1).astype(jnp.int32)
    scales = stacked(2)
    gathered = []
    for b in range(bands):
        onehot = jnp.where(col_ids == upright[:, b : b + 1].astype(jnp.int32), 1.0, 0.0).astype(BF16)
        pair = lax.shift_right_logical(levels[b * obs : (b + 1) * obs], 1)
        found = jnp.zeros((obs, LANES), F32)
        x_loads[b].wait()
        for p in range(0, pairs, 2):
            got = dot(onehot, x_v[b, :, p * LANES : (p + 2) * LANES])
            found = jnp.where(pair == p, got[:, :LANES], found)
            found = jnp.where(pair == p + 1, got[:, LANES:], found)
        gathered.append(found)
    found = jnp.concatenate(gathered, axis=0)
    total = bands * obs
    low_t = iota((total, LANES), 1) < K
    even = (levels & 1) == 0
    picked = jnp.where(low_t == even, found, pltpu.roll(found, K, 1))
    anomaly = picked - jnp.mean(picked, axis=1, keepdims=True)
    departs = (scales * (anomaly - stacked(3))).astype(BF16)
    own_ref[...] = departs
    wide = departs.astype(F32)
    centre = jnp.mean(wide, axis=1, keepdims=True)
    spread = wide - centre
    numerator = jnp.sum(centre * centre, axis=0, keepdims=True)
    spread_row = jnp.sum(spread * spread, axis=0, keepdims=True)
    mask_row = jnp.sum(mask, axis=0, keepdims=True)
    denominator = jnp.sum(spread_row, axis=1, keepdims=True) * (0.5 / (K - 1)) + jnp.sum(
        mask_row, axis=1, keepdims=True
    )
    stat_buf[me] = jnp.where(iota((1, LANES), 1) == 0, numerator, denominator)

    pl.semaphore_wait(barrier, devices - 1)

    def stat_copy(slot, step, other):
        return pltpu.make_async_remote_copy(
            src_ref=stat_buf.at[slot],
            dst_ref=stat_buf.at[slot],
            send_sem=stat_send.at[step],
            recv_sem=stat_recv.at[slot],
            device_id=other,
            device_id_type=MESH,
        )

    def near_copy(kind, slot, other):
        return pltpu.make_async_remote_copy(
            src_ref=ends_buf.at[kind],
            dst_ref=near_buf.at[slot],
            send_sem=near_send.at[slot],
            recv_sem=near_recv.at[slot],
            device_id=(lat, other),
            device_id_type=MESH,
        )

    def head_copy(other):
        return pltpu.make_async_remote_copy(
            src_ref=ends_buf.at[0],
            dst_ref=near_buf.at[2],
            send_sem=head_send.at[other],
            recv_sem=head_recv,
            device_id=(lat, other),
            device_id_type=MESH,
        )

    def tail_copy(slot):
        return pltpu.make_async_remote_copy(
            src_ref=ends_buf.at[2],
            dst_ref=tail_buf.at[slot],
            send_sem=tail_send,
            recv_sem=tail_recv.at[slot],
            device_id=(lat, 0),
            device_id_type=MESH,
        )

    def send_stat(step, carry):
        stat_copy(me, step, peer(step)).start()
        return carry

    lax.fori_loop(1, devices, send_stat, 0)

    low = iota((obs, LANES), 1) < K
    for q in range(bands // PAIR):
        mark = jnp.concatenate([marks[2 * q], marks[2 * q + 1]], axis=1)
        one = departs[(2 * q) * obs : (2 * q + 1) * obs]
        two = departs[(2 * q + 1) * obs : (2 * q + 2) * obs]
        both = jnp.concatenate(
            [jnp.where(low, one.astype(F32), 0.0), jnp.where(low, 0.0, two.astype(F32))], axis=0
        ).astype(BF16)
        compact = dot(mark, both).astype(BF16)
        for kind in range(3):
            ends_buf[kind, q] = compact[kind * ends : (kind + 1) * ends]

    @pl.when(lon > 0)
    def _():
        tail_copy(lon).start()
        near_copy(0, 1, lon - 1).start()

    @pl.when(lon == 0)
    def _():
        def send(other, carry):
            head_copy(other).start()
            return carry

        lax.fori_loop(1, lons, send, 0)

    @pl.when(lon < lons - 1)
    def _():
        near_copy(1, 0, lon + 1).start()

    tapering = taper_weights(RADIUS)
    slots = obs + 3 * ends
    lane = iota((1, LANES), 1)
    lane_band, lane_col = lane // columns, lane % columns
    count = jnp.zeros((1, LANES), jnp.int32)
    for b in range(bands):
        count = jnp.where(lane_band == b, cols_ref[b], count)
    chooser = jnp.where(iota((LANES, LANES), 0) == lane_band, 1.0, 0.0).astype(BF16)
    source = dot(upright.astype(BF16), chooser).astype(jnp.int32)
    source = jnp.concatenate([source, jnp.zeros((3 * ends, LANES), jnp.int32)], axis=0)
    place = iota((slots, LANES), 0)
    nth = (place - obs) // OC
    each = ends // OC
    source = jnp.where(
        place < obs,
        source,
        jnp.where(
            place < obs + ends,
            nth - reach,
            jnp.where(place < obs + 2 * ends, nth - each + columns, nth - 2 * each + count - first),
        ),
    )
    limit = jnp.where(place < obs, count, FAR)
    away = source - lane_col
    away = jnp.where(2 * away > limit, away - count, away)
    away = jnp.where(2 * away < -limit, away + count, away)
    away = jnp.abs(away)
    weight = jnp.zeros((slots, LANES), F32)
    for t in range(RADIUS):
        weight = jnp.where(away == t, tapering[t], weight)
    w_ref[...] = weight

    rows_x = xs.shape[0] // columns
    groups = columns // GROUP
    low_x = iota((rows_x, LANES), 1) < K
    xs[...] = jnp.zeros_like(xs)

    def spread_band(b, carry):
        for p in range(pairs):
            strip = x_v[b, :, p * LANES : (p + 1) * LANES].astype(F32)
            xs[pl.ds(p, columns, stride=rows_x), :] = strip
        for g in range(groups):
            halves = []
            for c in (g * GROUP, g * GROUP + 2):
                here = xs[c * rows_x : (c + 1) * rows_x, :]
                there = xs[(c + 1) * rows_x : (c + 2) * rows_x, :]
                halves.append(
                    jnp.concatenate(
                        [
                            jnp.where(low_x, here, pltpu.roll(there, K, 1)),
                            jnp.where(low_x, pltpu.roll(here, K, 1), there),
                        ],
                        axis=0,
                    ).astype(BF16)
                )
            xl_ref[b * groups + g] = jnp.concatenate(halves, axis=1)
        return carry

    lax.fori_loop(0, bands, spread_band, 0)

    @pl.when(lon > 0)
    def _():
        near_copy(1, 0, lon - 1).wait_recv()
        head_copy(lon).wait_recv()
        tail_copy(lon).wait_send()
        near_copy(0, 1, lon - 1).wait_send()

    @pl.when(lon == 0)
    def _():
        def take(other, carry):
            head_copy(other).wait_send()
            tail_copy(other).wait_recv()
            return carry

        lax.fori_loop(1, lons, take, 0)

    @pl.when(lon < lons - 1)
    def _():
        near_copy(0, 1, lon + 1).wait_recv()
        near_copy(1, 0, lon + 1).wait_send()

    side_ref[0] = (
        near_buf[0].astype(F32) + jnp.sum(tail_buf[...].astype(F32), axis=0)
    ).astype(BF16)
    side_ref[1] = near_buf[1]
    side_ref[2] = near_buf[2]

    def take_stat(step, carry):
        stat_copy(me, step, peer(step)).wait_send()
        source = lax.rem(me + devices - step, devices)
        stat_copy(source, step, peer(step)).wait_recv()
        return carry

    lax.fori_loop(1, devices, take_stat, 0)
    stats = jnp.sum(stat_buf[...], axis=0)
    inflation = (stats[:, 0:1] + 1e-06) / stats[:, 1:2]
    shift = jnp.broadcast_to((K - 1) / inflation, (8, LANES))
    line = iota((8, LANES), 0)
    info = shift
    for b in range(bands):
        info = jnp.where(line == 1 + b, (cols_ref[b] - first).astype(F32), info)
    info_ref[...] = info


def analysis_kernel(
    own_ref,
    side_ref,
    info_ref,
    w_ref,
    xl_ref,
    out_hbm,
    dc,
    lhs,
    cf,
    cb,
    sf,
    sb,
    nf,
    nb,
    xf,
    xb,
    tf,
    uf,
    px,
    ys,
    obuf,
    out_sem,
):
    bands, columns, width = obuf.shape
    obs = own_ref.shape[0] // bands
    ends = side_ref.shape[2]
    slots = obs + 3 * ends
    pairs = width // LANES
    groups = columns // GROUP
    rows_x = ys.shape[1] // columns
    tall = 2 * rows_x
    spare = pairs
    shift = info_ref[0:1, 0:1]
    low_b = jnp.where(iota((K, LANES), 1) < K, 1.0, 0.0).astype(BF16)
    high_b = jnp.where(iota((K, LANES), 1) < K, 0.0, 1.0).astype(BF16)
    zero_b = jnp.zeros((K, LANES), BF16)
    low_x = iota((rows_x, LANES), 1) < K
    eye = jnp.where(iota((K, SPAN), 0) == iota((K, SPAN), 1) % K, 1.0, 0.0)
    batch = [(j, g) for j in range(PAIR) for g in range(groups)]
    many = len(batch)

    def block_diag(mat):
        left, right = mat[:, :LANES], mat[:, LANES:]
        return jnp.concatenate(
            [
                jnp.concatenate([left * low_b, zero_b], axis=1),
                jnp.concatenate([left * high_b, zero_b], axis=1),
                jnp.concatenate([zero_b, right * low_b], axis=1),
                jnp.concatenate([zero_b, right * high_b], axis=1),
            ],
            axis=0,
        )

    ones_bd = block_diag(jnp.ones((K, SPAN), BF16))

    def one_pair(p, carry):
        sides = jnp.concatenate([side_ref[kind, p] for kind in range(3)], axis=0).astype(F32)
        swapped = pltpu.roll(sides, K, 1)
        low_s = iota((3 * ends, LANES), 1) < K
        low_h = iota((LANES, LANES), 1) < K
        for j in range(PAIR):
            start = pl.multiple_of((p * PAIR + j) * obs, obs)
            here = jnp.where(low_s, sides, swapped) if j == 0 else jnp.where(low_s, swapped, sides)
            slot = jnp.concatenate([own_ref[pl.ds(start, obs), :].astype(F32), here], axis=0)
            dc[j] = slot - jnp.mean(slot, axis=1, keepdims=True)
            rest = jnp.concatenate(
                [slot[LANES:], jnp.zeros((2 * LANES - slots, LANES), F32)], axis=0
            )
            turned = jnp.transpose(jnp.where(low_h, slot[:LANES], rest))
            turned = jnp.concatenate([turned[:K], turned[K:]], axis=1)
            centre = jnp.mean(turned, axis=0, keepdims=True)
            lhs[j] = jnp.concatenate(
                [turned - centre, -centre, jnp.zeros((15, SPAN), F32)], axis=0
            ).astype(BF16)

        squares = []
        lane_high = jnp.where(iota((slots, LANES), 1) < K, 0, 1)
        for i, (j, g) in enumerate(batch):
            right = []
            base = (p * PAIR + j) * columns + g * GROUP
            for half in range(2):
                index = lane_high + (base + 2 * half)
                spreadw = jnp.take_along_axis(w_ref[...], index, axis=1)
                right.append((dc[j] * spreadw).astype(BF16))
            gram = dot(lhs[j, :, :slots], jnp.concatenate(right, axis=1))
            c = gram[:K]
            cf[i] = c
            cb[i] = c.astype(BF16)
            mean = gram[K : K + 1]
            line = iota((16, SPAN), 0) + 16
            tile = xl_ref[(p * PAIR + j) * groups + g, 16:32, :].astype(F32)
            px[i] = jnp.where(line == spare, mean, tile).astype(BF16)
            system = c + shift * eye
            squares.append(jnp.sum(system * system, axis=0, keepdims=True))
        squares = jnp.concatenate(squares, axis=0)
        coarse = squares.astype(BF16)
        fine = (squares - coarse.astype(F32)).astype(BF16)
        sums = dot(jnp.concatenate([coarse, fine], axis=0), ones_bd)
        frob = jnp.sqrt(sums[:many] + sums[many:])
        inv = 1.0 / frob
        scaling = jnp.sqrt((K - 1.0) * inv)
        beta = 1.0 - shift * inv
        beta1 = beta * beta * (0.75 + 0.25 * beta)
        beta2 = beta1 * beta1 * (0.75 + 0.25 * beta1)
        k1 = -inv * (1.5 * beta + 0.75 * beta * beta)
        k2 = inv * inv * (0.75 + 0.75 * beta)
        k3 = -0.25 * inv * inv * inv
        a0 = 1.0 + 0.5 * beta
        d0 = -0.5 * inv
        a1 = 1.0 + 0.5 * beta1
        e1 = 1.5 * beta1 + 0.75 * beta1 * beta1
        e2 = 0.75 + 0.75 * beta1
        c0 = (1.0 + 0.5 * beta2) * (1.0 + (0.375 + 0.125 * beta2) * beta2 * beta2)
        c1 = 0.5 + beta2 * (0.75 + beta2 * (0.9375 + 0.25 * beta2))
        c2 = 0.375 + beta2 * (0.9375 + 0.375 * beta2)
        c3 = 0.3125 + 0.25 * beta2
        rest = (1.0 - scaling * a0 * a1 * c0) * (1.0 / K)

        def members(i, j, g):
            tile = (p * PAIR + j) * groups + g
            return jnp.concatenate(
                [xl_ref[tile, :16, :], px[i], xl_ref[tile, 32:, :]], axis=0
            )

        for i, (j, g) in enumerate(batch):
            both = dot(jnp.concatenate([cb[i], members(i, j, g)], axis=0), block_diag(cb[i]))
            square = both[:K]
            sf[i] = square
            sb[i] = square.astype(BF16)
            x1 = a0[i : i + 1] * members(i, j, g).astype(F32) + d0[i : i + 1] * both[K:]
            xf[i] = x1
            xb[i] = x1.astype(BF16)
        for i in range(many):
            cube = dot(cb[i], block_diag(sb[i]))
            dev = k1[i : i + 1] * cf[i] + k2[i : i + 1] * sf[i] + k3[i : i + 1] * cube
            nf[i] = dev
            nb[i] = dev.astype(BF16)
        for i in range(many):
            both = dot(jnp.concatenate([nb[i], xb[i]], axis=0), block_diag(nb[i]))
            square = both[:K]
            sf[i] = square
            sb[i] = square.astype(BF16)
            x2 = a1[i : i + 1] * xf[i] + 0.5 * both[K:]
            xf[i] = x2
            xb[i] = x2.astype(BF16)
        for i in range(many):
            cube = dot(nb[i], block_diag(sb[i]))
            dev = e1[i : i + 1] * nf[i] + e2[i : i + 1] * sf[i] + 0.25 * cube
            cb[i] = dev.astype(BF16)
        for i in range(many):
            both = dot(jnp.concatenate([cb[i], xb[i]], axis=0), block_diag(cb[i]))
            sb[i] = both[:K].astype(BF16)
            x2 = xf[i]
            tf[i] = c2[i : i + 1] * x2 + c3[i : i + 1] * both[K:]
            uf[i] = c0[i : i + 1] * x2 + c1[i : i + 1] * both[K:]
        for i in range(many):
            quad = dot(xb[i], block_diag(sb[i]))
            xb[i] = (tf[i] + 0.0625 * quad).astype(BF16)
        for i, (j, g) in enumerate(batch):
            x4 = uf[i] + dot(xb[i], block_diag(sb[i]))
            uf[i] = x4
            step = x4[spare : spare + 1] * inv[i : i + 1]
            xb[i] = (x4 * step + members(i, j, g).astype(F32) * rest[i : i + 1]).astype(BF16)
        for i, (j, g) in enumerate(batch):
            result = scaling[i : i + 1] * uf[i] + dot(xb[i], ones_bd)
            for side in range(2):
                c = g * GROUP + 2 * side
                got = result[:, side * LANES : (side + 1) * LANES]
                even, odd = got[:rows_x], got[rows_x:]
                ys[j, c * rows_x : (c + 1) * rows_x, :] = jnp.where(low_x, even, pltpu.roll(odd, K, 1))
                ys[j, (c + 1) * rows_x : (c + 2) * rows_x, :] = jnp.where(
                    low_x, pltpu.roll(even, K, 1), odd
                )
        for j in range(PAIR):
            b = p * PAIR + j
            keep = iota((columns, LANES), 0).astype(F32) < info_ref[pl.ds(1 + b, 1), :]
            for t in range(pairs):
                obuf[b, :, t * LANES : (t + 1) * LANES] = jnp.where(
                    keep, ys[j, pl.ds(t, columns, stride=rows_x), :], 0.0
                ).astype(BF16)
            pltpu.make_async_copy(obuf.at[b], out_hbm.at[b], out_sem.at[b]).start()
        return carry

    lax.fori_loop(0, bands // PAIR, one_pair, 0)
    for b in range(bands):
        pltpu.make_async_copy(obuf.at[b], out_hbm.at[b], out_sem.at[b]).wait()


def per_device(lats, lons, background, band_cols, obs_col, obs_lev, obs_mask, innov, obs_var):
    bands, columns, width = background.shape
    obs = obs_col.shape[1]
    pairs = width // LANES
    devices = lats * lons
    vmem = pl.BlockSpec(memory_space=pltpu.VMEM)
    hbm = pl.BlockSpec(memory_space=pltpu.HBM)
    dma = pltpu.SemaphoreType.DMA
    rows_x = -(-(pairs + 1) // 8) * 8
    halves = bands // PAIR
    slots = obs + 3 * END_SLOTS
    groups = columns // GROUP
    many = PAIR * groups
    room = 16 * 1024 * 1024
    own, side, info, weight, spread = pl.pallas_call(
        functools.partial(exchange_kernel, lats, lons),
        out_shape=(
            jax.ShapeDtypeStruct((bands * obs, LANES), BF16),
            jax.ShapeDtypeStruct((3, halves, END_SLOTS, LANES), BF16),
            jax.ShapeDtypeStruct((8, LANES), F32),
            jax.ShapeDtypeStruct((slots, LANES), F32),
            jax.ShapeDtypeStruct((bands * groups, 2 * rows_x, SPAN), BF16),
        ),
        in_specs=[hbm] * 7,
        out_specs=(vmem,) * 5,
        scratch_shapes=[
            pltpu.VMEM((bands, columns, width), BF16),
            pltpu.VMEM((bands, obs), jnp.int32),
            pltpu.VMEM((bands, obs), jnp.int32),
            pltpu.VMEM((bands, obs), jnp.int32),
            pltpu.VMEM((bands, obs), F32),
            pltpu.VMEM((bands, obs), F32),
            pltpu.SMEM((bands,), jnp.int32),
            pltpu.VMEM((columns * rows_x, LANES), F32),
            pltpu.VMEM((3, halves, END_SLOTS, LANES), BF16),
            pltpu.VMEM((3, halves, END_SLOTS, LANES), BF16),
            pltpu.VMEM((lons, halves, END_SLOTS, LANES), BF16),
            pltpu.VMEM((devices, 1, LANES), F32),
            dma((bands,)),
            dma((6,)),
            dma((2,)),
            dma((2,)),
            dma((lons,)),
            dma,
            dma,
            dma((lons,)),
            dma((devices,)),
            dma((devices,)),
        ],
        compiler_params=pltpu.CompilerParams(
            collective_id=0, has_side_effects=True, vmem_limit_bytes=room
        ),
        name="exchange",
    )(*(pltpu.with_memory_space_constraint(a, pltpu.HBM) for a in (background, obs_col, obs_lev, obs_mask, innov, obs_var, band_cols)))
    return pl.pallas_call(
        analysis_kernel,
        out_shape=jax.ShapeDtypeStruct(background.shape, BF16),
        in_specs=[vmem] * 5,
        out_specs=hbm,
        scratch_shapes=[
            pltpu.VMEM((PAIR, slots, LANES), F32),
            pltpu.VMEM((PAIR, K + 16, SPAN), BF16),
            pltpu.VMEM((many, K, SPAN), F32),
            pltpu.VMEM((many, K, SPAN), BF16),
            pltpu.VMEM((many, K, SPAN), F32),
            pltpu.VMEM((many, K, SPAN), BF16),
            pltpu.VMEM((many, K, SPAN), F32),
            pltpu.VMEM((many, K, SPAN), BF16),
            pltpu.VMEM((many, 2 * rows_x, SPAN), F32),
            pltpu.VMEM((many, 2 * rows_x, SPAN), BF16),
            pltpu.VMEM((many, 2 * rows_x, SPAN), F32),
            pltpu.VMEM((many, 2 * rows_x, SPAN), F32),
            pltpu.VMEM((many, 16, SPAN), BF16),
            pltpu.VMEM((PAIR, columns * rows_x, LANES), F32),
            pltpu.VMEM((bands, columns, width), BF16),
            dma((bands,)),
        ],
        compiler_params=pltpu.CompilerParams(vmem_limit_bytes=room),
        name="analysis",
    )(own, side, info, weight, spread)


def solution(mesh):
    placed = (P("lat", "lon", None), P("lat")) + (P("lat", "lon"),) * 5
    return jax.shard_map(
        functools.partial(per_device, mesh.shape["lat"], mesh.shape["lon"]),
        mesh=mesh,
        in_specs=placed,
        out_specs=P("lat", "lon", None),
        check_vma=False,
    )
```

time: 29.5 us -> 24 us (0.81)
  Pallas kernels: 29.3 us -> 23.8 us
    pallas_call x1, Pallas kernels: 14.3 us -> 11.3 us  [per_device(): pl.pallas_call(analysis_kernel, out_shape=jax.ShapeDtypeStruct(background...]
    pallas_call x1, Pallas kernels: 15 us -> 12.5 us  [per_device(): pl.pallas_call(functools.partial(exchange_kernel, lats, lons), out_shape=...]
where the time goes in v1:
time: 24 us; the launch traced here: 23.8 us
  Pallas kernels  23.8 us (99%)
    pallas_call x1, Pallas kernels, per_device(): pl.pallas_call(functools.partial(exchange_kernel, lats, lons), out_shape=...  12.5 us
    pallas_call x1, Pallas kernels, per_device(): pl.pallas_call(analysis_kernel, out_shape=jax.ShapeDtypeStruct(background...  11.3 us

profile of v1, /device:TPU:0, one launch (start us, length us, event | category | flops | bytes accessed | tf_op | source)
XLA Modules:
  0.0 23.8 jit_solution(3242499179785892269)
XLA Ops:
  0.0 12.5 %exchange.1 = (bf16[256,128]{1,0:T(8,128)(2,1)S(1)}, bf16[3,2,32,128]{3,2,1,0:T(8,128)(2,1)S(1)}, f32[8,128]{1,0:T(8,128)S(1)}, f32[160,128]{1,0:T(8,128)S(1)}, bf16[32,48,256]{2,1,0:T(8,128)(2,1)S(1)}) custom-call(bf16[4,32,2560]{2,1,0:T(8,128)(2,1)} %x_hbm.1, s32[4,64]{1,0:T(4,128)} %col_hbm.1, s32[4,64]{1,0:T(4,128)} %lev_hbm.1, s32[4,64]{1,0:T(4,128)} %mask_hbm.1, ...), custom_call_target="tpu_custom_call" | custom-call | tf_op jit(solution)/shard_map/exchange/pallas_call | solution.py:581
  12.5 11.3 %analysis.1 = bf16[4,32,2560]{2,1,0:T(8,128)(2,1)} custom-call(bf16[256,128]{1,0:T(8,128)(2,1)S(1)} %get-tuple-element.10.own_ref, bf16[3,2,32,128]{3,2,1,0:T(8,128)(2,1)S(1)} %get-tuple-element.11.side_ref, f32[8,128]{1,0:T(8,128)S(1)} %get-tuple-element.12.info_ref, f32[160,128]{1,0:T(8,128)S(1)} %get-tuple-element.13.w_ref, ...), custom_call_target="tpu_custom_call" | custom-call | tf_op jit(solution)/shard_map/analysis/pallas_call | solution.py:621

commit v2 on v1

v2 whole, which is shorter than its diff:
```python
import functools

import jax
import jax.numpy as jnp
from jax import lax
from jax.experimental import pallas as pl
from jax.experimental.pallas import tpu as pltpu
from jax.sharding import PartitionSpec as P

K = 64
RADIUS = 8
GROUP = 4
OC = 4
END_SLOTS = 32
FAR = 1 << 20
LANES = 128
PAIR = 2
SPAN = GROUP * K
F32 = jnp.float32
BF16 = jnp.bfloat16
MESH = pl.DeviceIdType.MESH


def taper_weights(radius):
    half_width = radius / 2.0
    tapering = []
    for offset in range(radius):
        distance = offset / half_width
        if distance <= 1.0:
            weight = (
                ((-0.25 * distance + 0.5) * distance + 0.625) * distance**3
                - 5.0 / 3.0 * distance**2
                + 1.0
            )
        else:
            weight = (
                (((distance / 12.0 - 0.5) * distance + 0.625) * distance + 5.0 / 3.0) * distance**2
                - 5.0 * distance
                + 4.0
                - 2.0 / (3.0 * distance)
            )
        tapering.append(weight)
    return tapering


def dot(left, right):
    return jnp.dot(left, right, preferred_element_type=F32)


def iota(shape, dim):
    return lax.broadcasted_iota(jnp.int32, shape, dim)


def block_diag(mat):
    lanes = iota((K, LANES), 1)
    low = jnp.where(lanes < K, 1.0, 0.0).astype(BF16)
    high = jnp.where(lanes < K, 0.0, 1.0).astype(BF16)
    zero = jnp.zeros((K, LANES), BF16)
    left, right = mat[:, :LANES], mat[:, LANES:]
    return jnp.concatenate(
        [
            jnp.concatenate([left * low, zero], axis=1),
            jnp.concatenate([left * high, zero], axis=1),
            jnp.concatenate([zero, right * low], axis=1),
            jnp.concatenate([zero, right * high], axis=1),
        ],
        axis=0,
    )


def exchange_kernel(
    lats,
    lons,
    x_hbm,
    col_hbm,
    lev_hbm,
    mask_hbm,
    innov_hbm,
    var_hbm,
    cols_hbm,
    c_out,
    s_out,
    q_out,
    p_out,
    x_out,
    norm_out,
    info_out,
    x_v,
    col_ref,
    lev_ref,
    mask_ref,
    innov_ref,
    var_ref,
    cols_ref,
    xs,
    own,
    weights,
    ends_buf,
    near_buf,
    tail_buf,
    stat_buf,
    x_sem,
    in_sem,
    near_send,
    near_recv,
    head_send,
    head_recv,
    tail_send,
    tail_recv,
    stat_send,
    stat_recv,
):
    lat, lon = lax.axis_index("lat"), lax.axis_index("lon")
    bands, columns, width = x_v.shape
    obs = col_ref.shape[1]
    devices = lats * lons
    me = lat * lons + lon
    smalls = (
        (col_hbm, col_ref),
        (lev_hbm, lev_ref),
        (mask_hbm, mask_ref),
        (innov_hbm, innov_ref),
        (var_hbm, var_ref),
        (cols_hbm, cols_ref),
    )
    loads = [
        pltpu.make_async_copy(source, target, in_sem.at[i])
        for i, (source, target) in enumerate(smalls)
    ]
    x_loads = [pltpu.make_async_copy(x_hbm.at[b], x_v.at[b], x_sem.at[b]) for b in range(bands)]
    for load in loads + x_loads:
        load.start()
    barrier = pltpu.get_barrier_semaphore()
    near_buf[...] = jnp.zeros_like(near_buf)
    tail_buf[...] = jnp.zeros_like(tail_buf)

    for other in range(devices):

        @pl.when(me != other)
        def _():
            pl.semaphore_signal(
                barrier, inc=1, device_id=(other // lons, other % lons), device_id_type=MESH
            )

    pairs = width // LANES
    reach = RADIUS - 1
    ends = END_SLOTS
    first = lon * columns
    for load in loads:
        load.wait()
    mask = mask_ref[...].astype(F32)
    used_all = mask > 0.0
    local_int = jnp.where(used_all, col_ref[...] - first, -columns)
    local = local_int.astype(F32)
    lev = lev_ref[...]
    spot = (lax.shift_right_logical(lev, 1) * columns + col_ref[...] - first) * 2 + (lev & 1)
    scale = jnp.sqrt(mask / var_ref[...])
    params = jnp.concatenate([local, spot.astype(F32), scale, innov_ref[...]], axis=0)
    params = jnp.concatenate([params, jnp.zeros((LANES - 4 * bands, obs), F32)], axis=0)
    params = jnp.concatenate([params, jnp.zeros((LANES, LANES - obs), F32)], axis=1)
    upright = jnp.transpose(params)[:obs]
    earlier = iota((obs, obs), 0) < iota((obs, obs), 1)
    slot_ids = iota((ends, obs), 0)

    def stacked(kind):
        return jnp.concatenate(
            [upright[:, kind * bands + b : kind * bands + b + 1] for b in range(bands)], axis=0
        )

    marks = []
    for b in range(bands):
        row = local_int[b : b + 1]
        used = used_all[b : b + 1]
        same = (upright[:, b : b + 1] == local[b : b + 1]) & earlier
        rank = jnp.sum(jnp.where(same, 1.0, 0.0), axis=0, keepdims=True).astype(jnp.int32)
        bases = (row, row - (columns - reach), row + first - (cols_ref[b] - reach))
        mark = []
        for base in bases:
            fits = used & (base >= 0) & (base < reach)
            slot = jnp.where(fits, base * OC + rank, -1)
            mark.append(jnp.where(slot_ids == slot, 1.0, 0.0))
        marks.append(jnp.concatenate(mark, axis=0).astype(BF16))

    spots = stacked(1).astype(jnp.int32)
    scales = stacked(2)
    depth = pairs * columns
    gathered = []
    for b in range(bands):
        index = lax.shift_right_logical(spots[b * obs : (b + 1) * obs], 1)
        onehot = jnp.where(iota((obs, depth), 1) == index, 1.0, 0.0).astype(BF16)
        x_loads[b].wait()
        field = jnp.concatenate(
            [x_v[b, :, p * LANES : (p + 1) * LANES] for p in range(pairs)], axis=0
        )
        gathered.append(dot(onehot, field))
    found = jnp.concatenate(gathered, axis=0)
    total = bands * obs
    low_t = iota((total, LANES), 1) < K
    even = (spots & 1) == 0
    picked = jnp.where(low_t == even, found, pltpu.roll(found, K, 1))
    anomaly = picked - jnp.mean(picked, axis=1, keepdims=True)
    departs = (scales * (anomaly - stacked(3))).astype(BF16)
    wide = departs.astype(F32)
    own[...] = wide
    centre = jnp.mean(wide, axis=1, keepdims=True)
    spread = wide - centre
    numerator = jnp.sum(centre * centre, axis=0, keepdims=True)
    spread_row = jnp.sum(spread * spread, axis=0, keepdims=True)
    mask_row = jnp.sum(mask, axis=0, keepdims=True)
    denominator = jnp.sum(spread_row, axis=1, keepdims=True) * (0.5 / (K - 1)) + jnp.sum(
        mask_row, axis=1, keepdims=True
    )
    stat_buf[me] = jnp.where(iota((1, LANES), 1) == 0, numerator, denominator)

    pl.semaphore_wait(barrier, devices - 1)

    def stat_copy(slot, size, other):
        return pltpu.make_async_remote_copy(
            src_ref=stat_buf.at[pl.ds(slot, size)],
            dst_ref=stat_buf.at[pl.ds(slot, size)],
            send_sem=stat_send,
            recv_sem=stat_recv,
            device_id=(other // lons, other % lons),
            device_id_type=MESH,
        )

    def near_copy(kind, slot, other):
        return pltpu.make_async_remote_copy(
            src_ref=ends_buf.at[kind],
            dst_ref=near_buf.at[slot],
            send_sem=near_send.at[slot],
            recv_sem=near_recv.at[slot],
            device_id=(lat, other),
            device_id_type=MESH,
        )

    def head_copy(other):
        return pltpu.make_async_remote_copy(
            src_ref=ends_buf.at[0],
            dst_ref=near_buf.at[2],
            send_sem=head_send.at[other],
            recv_sem=head_recv,
            device_id=(lat, other),
            device_id_type=MESH,
        )

    def tail_copy(slot):
        return pltpu.make_async_remote_copy(
            src_ref=ends_buf.at[2],
            dst_ref=tail_buf.at[slot],
            send_sem=tail_send,
            recv_sem=tail_recv,
            device_id=(lat, 0),
            device_id_type=MESH,
        )

    for other in range(devices):

        @pl.when(me != other)
        def _():
            stat_copy(me, 1, other).start()

    low = iota((obs, LANES), 1) < K
    for q in range(bands // PAIR):
        mark = jnp.concatenate([marks[2 * q], marks[2 * q + 1]], axis=1)
        one = wide[(2 * q) * obs : (2 * q + 1) * obs]
        two = wide[(2 * q + 1) * obs : (2 * q + 2) * obs]
        both = jnp.concatenate(
            [jnp.where(low, one, 0.0), jnp.where(low, 0.0, two)], axis=0
        ).astype(BF16)
        compact = dot(mark, both).astype(BF16)
        for kind in range(3):
            ends_buf[kind, q] = compact[kind * ends : (kind + 1) * ends]

    @pl.when(lon > 0)
    def _():
        tail_copy(lon).start()
        near_copy(0, 1, lon - 1).start()

    @pl.when(lon == 0)
    def _():
        for other in range(1, lons):
            head_copy(other).start()

    @pl.when(lon < lons - 1)
    def _():
        near_copy(1, 0, lon + 1).start()

    tapering = taper_weights(RADIUS)
    slots = obs + 2 * ends
    lane = iota((1, LANES), 1)
    lane_band, lane_col = lane // columns, lane % columns
    count = jnp.zeros((1, LANES), jnp.int32)
    for b in range(bands):
        count = jnp.where(lane_band == b, cols_ref[b], count)
    chooser = jnp.where(iota((LANES, LANES), 0) == lane_band, 1.0, 0.0).astype(BF16)
    source = dot(upright.astype(BF16), chooser).astype(jnp.int32)
    nth = iota((ends, LANES), 0) // OC

    def taper(place, limit):
        away = place - lane_col
        away = jnp.where(2 * away > limit, away - limit, away)
        away = jnp.where(2 * away < -limit, away + limit, away)
        away = jnp.abs(away)
        weight = jnp.zeros(place.shape, F32)
        for t in range(RADIUS):
            weight = jnp.where(away == t, tapering[t], weight)
        return weight.astype(BF16)

    near_own = taper(source, count)
    near_left = taper(nth - reach, FAR)
    near_right = taper(nth + columns, FAR)
    near_head = taper(nth + count - first, FAR)
    weights[0] = jnp.concatenate([near_own, near_right, near_head], axis=0)
    weights[1] = jnp.concatenate([near_own, near_left, near_head], axis=0)

    rows_x = xs.shape[0] // columns
    groups = columns // GROUP
    low_x = iota((rows_x, LANES), 1) < K
    xs[...] = jnp.zeros_like(xs)

    def spread_band(b, carry):
        for p in range(pairs):
            strip = x_v[b, :, p * LANES : (p + 1) * LANES].astype(F32)
            xs[pl.ds(p, columns, stride=rows_x), :] = strip
        for g in range(groups):
            halves = []
            for c in (g * GROUP, g * GROUP + 2):
                here = xs[c * rows_x : (c + 1) * rows_x, :]
                there = xs[(c + 1) * rows_x : (c + 2) * rows_x, :]
                halves.append(
                    jnp.concatenate(
                        [
                            jnp.where(low_x, here, pltpu.roll(there, K, 1)),
                            jnp.where(low_x, pltpu.roll(here, K, 1), there),
                        ],
                        axis=0,
                    ).astype(BF16)
                )
            x_out[b * groups + g] = jnp.concatenate(halves, axis=1)
        return carry

    lax.fori_loop(0, bands, spread_band, 0)

    eye = jnp.where(iota((K, SPAN), 0) == iota((K, SPAN), 1) % K, 1.0, 0.0)
    low_e = iota((2 * ends, LANES), 1) < K
    spare = pairs
    expand_row = iota((LANES, SPAN), 0) - iota((LANES, SPAN), 1) // K
    row_id = iota((16, SPAN), 0) + 16

    def early(p, which, chosen, extra):
        swapped = pltpu.roll(extra, K, 1)
        made = []
        for j in range(PAIR):
            b = p * PAIR + j
            here = jnp.where(low_e, extra, swapped) if j == 0 else jnp.where(low_e, swapped, extra)
            mine = own[pl.ds(pl.multiple_of(b * obs, obs), obs), :]
            slot = jnp.concatenate([mine, here], axis=0)
            spread = slot - jnp.mean(slot, axis=1, keepdims=True)
            turned = jnp.transpose(slot)[:K]
            centre = jnp.mean(turned, axis=0, keepdims=True)
            left = jnp.concatenate(
                [turned - centre, -centre, jnp.zeros((15, slots), F32)], axis=0
            ).astype(BF16)
            made.append((left, spread))
        places = [(j, g) for j in range(PAIR) for g in chosen]
        at = [(p * PAIR + j) * groups + g for j, g in places]
        right = []
        for j, g in places:
            picker = jnp.where(
                expand_row == (p * PAIR + j) * columns + g * GROUP, 1.0, 0.0
            ).astype(BF16)
            wide_w = dot(weights[which], picker)
            spread = made[j][1]
            right.append(
                jnp.concatenate(
                    [
                        (spread * wide_w[:, :LANES]).astype(BF16),
                        (spread * wide_w[:, LANES:]).astype(BF16),
                    ],
                    axis=1,
                )
            )
        narrow, fields = [], []
        for (j, g), i, r in zip(places, at, right):
            gram = dot(made[j][0], r)
            c = gram[:K]
            c_out[i] = c
            narrow.append(c.astype(BF16))
            mean = gram[K : K + 1]
            old = x_out[i]
            middle = jnp.where(row_id == spare, mean, old[16:32].astype(F32)).astype(BF16)
            field = jnp.concatenate([old[:16], middle, old[32:]], axis=0)
            x_out[i] = field
            fields.append(field)
            norm_out[0, pl.ds(i, 1), :] = jnp.sum(c * c, axis=0, keepdims=True)
            norm_out[1, pl.ds(i, 1), :] = jnp.sum(c * eye, axis=0, keepdims=True)
        squares = []
        for i, n, f in zip(at, narrow, fields):
            both = dot(jnp.concatenate([n, f], axis=0), block_diag(n))
            s_out[i] = both[:K]
            p_out[i] = both[K:]
            squares.append(both[:K].astype(BF16))
        for i, n, q in zip(at, narrow, squares):
            q_out[i] = dot(n, block_diag(q))

    @pl.when(lon > 0)
    def _():
        head_copy(lon).wait_recv()

    @pl.when(lon < lons - 1)
    def _():
        near_copy(0, 1, lon + 1).wait_recv()

    edge = -(-reach // GROUP)

    def inner(p, carry):
        extra = jnp.concatenate([near_buf[1, p], near_buf[2, p]], axis=0).astype(F32)
        early(p, 0, range(edge, groups), extra)
        return carry

    lax.fori_loop(0, bands // PAIR, inner, 0)

    @pl.when(lon > 0)
    def _():
        near_copy(1, 0, lon - 1).wait_recv()

    @pl.when(lon == 0)
    def _():
        pltpu.make_async_remote_copy(
            src_ref=tail_buf.at[pl.ds(1, lons - 1)],
            dst_ref=tail_buf.at[pl.ds(1, lons - 1)],
            send_sem=tail_send,
            recv_sem=tail_recv,
            device_id=(lat, 0),
            device_id_type=MESH,
        ).wait_recv()

    def outer(p, carry):
        ahead = near_buf[0, p].astype(F32)
        for other in range(1, lons):
            ahead = ahead + tail_buf[other, p].astype(F32)
        extra = jnp.concatenate([ahead, near_buf[2, p].astype(F32)], axis=0)
        early(p, 1, range(edge), extra)
        return carry

    lax.fori_loop(0, bands // PAIR, outer, 0)

    @pl.when(lon > 0)
    def _():
        tail_copy(lon).wait_send()
        near_copy(0, 1, lon - 1).wait_send()

    @pl.when(lon == 0)
    def _():
        for other in range(1, lons):
            head_copy(other).wait_send()

    @pl.when(lon < lons - 1)
    def _():
        near_copy(1, 0, lon + 1).wait_send()

    everyone = stat_copy(0, devices - 1, 0)
    everyone.wait_send()
    everyone.wait_recv()
    stats = jnp.sum(stat_buf[...], axis=0)
    inflation = (stats[:, 0:1] + 1e-06) / stats[:, 1:2]
    shift = jnp.broadcast_to((K - 1) / inflation, (8, LANES))
    line = iota((8, LANES), 0)
    info = shift
    for b in range(bands):
        info = jnp.where(line == 1 + b, (cols_ref[b] - first).astype(F32), info)
    info_out[...] = info


def analysis_kernel(
    c_ref,
    s_ref,
    q_ref,
    p_ref,
    x_ref,
    norm_ref,
    info_ref,
    out_hbm,
    coef,
    ys,
    obuf,
    out_sem,
):
    bands, columns, width = obuf.shape
    pairs = width // LANES
    groups = columns // GROUP
    rows_x = ys.shape[1] // columns
    spare = pairs
    shift = info_ref[0:1, 0:1]
    low_x = iota((rows_x, LANES), 1) < K
    batch = [(j, g) for j in range(PAIR) for g in range(groups)]
    many = len(batch)
    ones_bd = block_diag(jnp.ones((K, SPAN), BF16))

    squares = norm_ref[0] + shift * (2.0 * norm_ref[1] + shift)
    coarse = squares.astype(BF16)
    fine = (squares - coarse.astype(F32)).astype(BF16)
    sums = dot(jnp.concatenate([coarse, fine], axis=0), ones_bd)
    size = squares.shape[0]
    inv = lax.rsqrt(sums[:size] + sums[size:])
    scaling = jnp.sqrt((K - 1.0) * inv)
    beta = 1.0 - shift * inv
    beta1 = beta * beta * (0.75 + 0.25 * beta)
    beta2 = beta1 * beta1 * (0.75 + 0.25 * beta1)
    a0 = 1.0 + 0.5 * beta
    a1 = 1.0 + 0.5 * beta1
    half1 = 0.5 / a1
    c0 = (1.0 + 0.5 * beta2) * (1.0 + (0.375 + 0.125 * beta2) * beta2 * beta2)
    c1 = 0.5 + beta2 * (0.75 + beta2 * (0.9375 + 0.25 * beta2))
    c2 = 0.375 + beta2 * (0.9375 + 0.375 * beta2)
    c3 = 0.3125 + 0.25 * beta2
    up, down = c1 / c0, c0 / c1
    whole = a0 * a1 * c0
    table = (
        -inv * (1.5 * beta + 0.75 * beta * beta) * half1,
        inv * inv * (0.75 + 0.75 * beta) * half1,
        -0.25 * inv * inv * inv * half1,
        -0.5 * inv / a0,
        2.0 * a1 * up * (1.5 * beta1 + 0.75 * beta1 * beta1),
        4.0 * a1 * a1 * up * (0.75 + 0.75 * beta1),
        2.0 * a1 * a1 * a1 * up,
        c2 / c0 * down * down,
        c3 / c0 * down * down * down,
        0.0625 / c0 * (down * down) * (down * down),
        whole * whole * inv,
        (1.0 - scaling * whole) * (1.0 / K),
        scaling * whole,
    )
    for t, value in enumerate(table):
        coef[t] = value

    def one_pair(p, carry):
        at = [(p * PAIR + j) * groups + g for j, g in batch]

        def k(t, i):
            return coef[t, pl.ds(i, 1), :]

        def wide_x(i):
            return x_ref[i].astype(F32)

        dev, dev_b, mem, mem_b = [], [], [], []
        for i in at:
            m = k(0, i) * c_ref[i] + k(1, i) * s_ref[i] + k(2, i) * q_ref[i]
            x = wide_x(i) + k(3, i) * p_ref[i]
            dev.append(m)
            dev_b.append(m.astype(BF16))
            mem.append(x)
            mem_b.append(x.astype(BF16))
        both = [
            dot(jnp.concatenate([n, x], axis=0), block_diag(n)) for n, x in zip(dev_b, mem_b)
        ]
        square = [v[:K] for v in both]
        mem = [x + v[K:] for x, v in zip(mem, both)]
        cube = [dot(n, block_diag(s.astype(BF16))) for n, s in zip(dev_b, square)]
        dev_b = [
            (k(4, i) * n + k(5, i) * s + k(6, i) * q).astype(BF16)
            for i, n, s, q in zip(at, dev, square, cube)
        ]
        mem_b = [x.astype(BF16) for x in mem]
        both = [
            dot(jnp.concatenate([n, x], axis=0), block_diag(n)) for n, x in zip(dev_b, mem_b)
        ]
        fixed = [v[:K].astype(BF16) for v in both]
        part = [
            k(7, i) * x + k(8, i) * v[K:] for i, x, v in zip(at, mem, both)
        ]
        mem = [x + v[K:] for x, v in zip(mem, both)]
        quad = [dot(x, block_diag(f)) for x, f in zip(mem_b, fixed)]
        part = [
            (y + k(9, i) * v).astype(BF16) for i, y, v in zip(at, part, quad)
        ]
        mem = [x + dot(y, block_diag(f)) for x, y, f in zip(mem, part, fixed)]
        mean_b = [
            (x * (x[spare : spare + 1] * k(10, i)) + wide_x(i) * k(11, i)).astype(BF16)
            for i, x in zip(at, mem)
        ]
        for i, (j, g), x, m in zip(at, batch, mem, mean_b):
            result = k(12, i) * x + dot(m, ones_bd)
            for side in range(2):
                c = g * GROUP + 2 * side
                got = result[:, side * LANES : (side + 1) * LANES]
                even, odd = got[:rows_x], got[rows_x:]
                ys[j, c * rows_x : (c + 1) * rows_x, :] = jnp.where(low_x, even, pltpu.roll(odd, K, 1))
                ys[j, (c + 1) * rows_x : (c + 2) * rows_x, :] = jnp.where(
                    low_x, pltpu.roll(even, K, 1), odd
                )
        for j in range(PAIR):
            b = p * PAIR + j
            keep = iota((columns, LANES), 0).astype(F32) < info_ref[pl.ds(1 + b, 1), :]
            for t in range(pairs):
                obuf[b, :, t * LANES : (t + 1) * LANES] = jnp.where(
                    keep, ys[j, pl.ds(t, columns, stride=rows_x), :], 0.0
                ).astype(BF16)
            pltpu.make_async_copy(obuf.at[b], out_hbm.at[b], out_sem.at[b]).start()
        return carry

    lax.fori_loop(0, bands // PAIR, one_pair, 0)
    for b in range(bands):
        pltpu.make_async_copy(obuf.at[b], out_hbm.at[b], out_sem.at[b]).wait()


def per_device(lats, lons, background, band_cols, obs_col, obs_lev, obs_mask, innov, obs_var):
    bands, columns, width = background.shape
    obs = obs_col.shape[1]
    pairs = width // LANES
    devices = lats * lons
    vmem = pl.BlockSpec(memory_space=pltpu.VMEM)
    hbm = pl.BlockSpec(memory_space=pltpu.HBM)
    dma = pltpu.SemaphoreType.DMA
    rows_x = -(-(pairs + 1) // 8) * 8
    halves = bands // PAIR
    slots = obs + 2 * END_SLOTS
    total = bands * columns // GROUP
    room = 16 * 1024 * 1024
    arrays = (background, obs_col, obs_lev, obs_mask, innov, obs_var, band_cols)
    made = pl.pallas_call(
        functools.partial(exchange_kernel, lats, lons),
        out_shape=(
            jax.ShapeDtypeStruct((total, K, SPAN), F32),
            jax.ShapeDtypeStruct((total, K, SPAN), F32),
            jax.ShapeDtypeStruct((total, K, SPAN), F32),
            jax.ShapeDtypeStruct((total, 2 * rows_x, SPAN), F32),
            jax.ShapeDtypeStruct((total, 2 * rows_x, SPAN), BF16),
            jax.ShapeDtypeStruct((2, total, SPAN), F32),
            jax.ShapeDtypeStruct((8, LANES), F32),
        ),
        in_specs=[hbm] * 7,
        out_specs=(vmem,) * 7,
        scratch_shapes=[
            pltpu.VMEM((bands, columns, width), BF16),
            pltpu.VMEM((bands, obs), jnp.int32),
            pltpu.VMEM((bands, obs), jnp.int32),
            pltpu.VMEM((bands, obs), jnp.int32),
            pltpu.VMEM((bands, obs), F32),
            pltpu.VMEM((bands, obs), F32),
            pltpu.SMEM((bands,), jnp.int32),
            pltpu.VMEM((columns * rows_x, LANES), F32),
            pltpu.VMEM((bands * obs, LANES), F32),
            pltpu.VMEM((2, slots, LANES), BF16),
            pltpu.VMEM((3, halves, END_SLOTS, LANES), BF16),
            pltpu.VMEM((3, halves, END_SLOTS, LANES), BF16),
            pltpu.VMEM((lons, halves, END_SLOTS, LANES), BF16),
            pltpu.VMEM((devices, 1, LANES), F32),
            dma((bands,)),
            dma((6,)),
            dma((2,)),
            dma((2,)),
            dma((lons,)),
            dma,
            dma,
            dma,
            dma,
            dma,
        ],
        compiler_params=pltpu.CompilerParams(
            collective_id=0, has_side_effects=True, vmem_limit_bytes=room
        ),
        name="exchange",
    )(*(pltpu.with_memory_space_constraint(a, pltpu.HBM) for a in arrays))
    return pl.pallas_call(
        analysis_kernel,
        out_shape=jax.ShapeDtypeStruct(background.shape, BF16),
        in_specs=[vmem] * 7,
        out_specs=hbm,
        scratch_shapes=[
            pltpu.VMEM((13, total, SPAN), F32),
            pltpu.VMEM((PAIR, columns * rows_x, LANES), F32),
            pltpu.VMEM((bands, columns, width), BF16),
            dma((bands,)),
        ],
        compiler_params=pltpu.CompilerParams(vmem_limit_bytes=room),
        name="analysis",
    )(*made)


def solution(mesh):
    placed = (P("lat", "lon", None), P("lat")) + (P("lat", "lon"),) * 5
    return jax.shard_map(
        functools.partial(per_device, mesh.shape["lat"], mesh.shape["lon"]),
        mesh=mesh,
        in_specs=placed,
        out_specs=P("lat", "lon", None),
        check_vma=False,
    )
```

time: 24 us -> 20.8 us (0.87)
  Pallas kernels: 23.8 us -> 20.6 us
    pallas_call x1, Pallas kernels: 11.3 us -> 5.94 us  [per_device(): pl.pallas_call(analysis_kernel, out_shape=jax.ShapeDtypeStruct(background...]
    pallas_call x1, Pallas kernels: 12.5 us -> 14.7 us  [per_device(): pl.pallas_call(functools.partial(exchange_kernel, lats, lons), out_shape=...]
where the time goes in v2:
time: 20.8 us; the launch traced here: 20.7 us
  Pallas kernels  20.6 us (99%)
    pallas_call x1, Pallas kernels, per_device(): pl.pallas_call(functools.partial(exchange_kernel, lats, lons), out_shape=...  14.7 us
    pallas_call x1, Pallas kernels, per_device(): pl.pallas_call(analysis_kernel, out_shape=jax.ShapeDtypeStruct(background...  5.94 us

profile of v2, /device:TPU:0, one launch (start us, length us, event | category | flops | bytes accessed | tf_op | source)
XLA Modules:
  0.0 20.7 jit_solution(11344370095705167042)
XLA Ops:
  0.0 14.7 %exchange.1 = (f32[32,64,256]{2,1,0:T(8,128)S(1)}, f32[32,64,256]{2,1,0:T(8,128)S(1)}, f32[32,64,256]{2,1,0:T(8,128)S(1)}, f32[32,48,256]{2,1,0:T(8,128)S(1)}, b...) custom-call(bf16[4,32,2560]{2,1,0:T(8,128)(2,1)} %x_hbm.1, s32[4,64]{1,0:T(4,128)} %col_hbm.1, ...), custom_call_target="tpu_custom_call" | custom-call | tf_op jit(solution)/shard_map/exchange/pallas_call | solution.py:622
  14.7 5.9 %analysis.1 = bf16[4,32,2560]{2,1,0:T(8,128)(2,1)} custom-call(f32[32,64,256]{2,1,0:T(8,128)S(1)} %get-tuple-element.12.c_ref, f32[32,64,256]{2,1,0:T(8,128)S(1)} %get-tuple-element.13.s_ref, f32[32,64,256]{2,1,0:T(8,128)S(1)} %get-tuple-element.14.q_ref, f32[32,48,256]{2,1,0:T(8,128)S(1)} %get-tuple-element.15.p_ref, ...), custom_call_target="tpu_custom_call" | custom-call | tf_op jit(solution)/shard_map/analysis/pallas_call | solution.py:666

commit v3 on v2

v3 whole, which is shorter than its diff:
```python
import functools

import jax
import jax.numpy as jnp
from jax import lax
from jax.experimental import pallas as pl
from jax.experimental.pallas import tpu as pltpu
from jax.sharding import PartitionSpec as P

K = 64
RADIUS = 8
GROUP = 4
OC = 4
END_SLOTS = 32
FAR = 1 << 20
GAP_OWN = 16
GAP_EARLY = 12
GAP_LATE = 8
SHARED = 4
LANES = 128
PAIR = 2
SPAN = GROUP * K
F32 = jnp.float32
BF16 = jnp.bfloat16
MESH = pl.DeviceIdType.MESH


def taper_weights(radius):
    half_width = radius / 2.0
    tapering = []
    for offset in range(radius):
        distance = offset / half_width
        if distance <= 1.0:
            weight = (
                ((-0.25 * distance + 0.5) * distance + 0.625) * distance**3
                - 5.0 / 3.0 * distance**2
                + 1.0
            )
        else:
            weight = (
                (((distance / 12.0 - 0.5) * distance + 0.625) * distance + 5.0 / 3.0) * distance**2
                - 5.0 * distance
                + 4.0
                - 2.0 / (3.0 * distance)
            )
        tapering.append(weight)
    return tapering


def dot(left, right):
    return jnp.dot(left, right, preferred_element_type=F32)


def iota(shape, dim):
    return lax.broadcasted_iota(jnp.int32, shape, dim)


def block_diag(mat):
    lanes = iota((K, LANES), 1)
    zero = jnp.zeros((K, LANES), BF16)
    left, right = mat[:, :LANES], mat[:, LANES:]
    return jnp.concatenate(
        [
            jnp.concatenate([jnp.where(lanes < K, left, zero), zero], axis=1),
            jnp.concatenate([jnp.where(lanes < K, zero, left), zero], axis=1),
            jnp.concatenate([zero, jnp.where(lanes < K, right, zero)], axis=1),
            jnp.concatenate([zero, jnp.where(lanes < K, zero, right)], axis=1),
        ],
        axis=0,
    )


def wavefront(tasks, gap):
    started = []
    step = 0
    while step < len(tasks) or started:
        if step < len(tasks):
            started.append((step, tasks[step]))
        left = []
        for begin, task in started:
            if (step - begin) % gap == 0:
                try:
                    next(task)
                except StopIteration:
                    continue
            left.append((begin, task))
        started = left
        step += 1


def exchange_kernel(
    lats,
    lons,
    x_hbm,
    col_hbm,
    lev_hbm,
    mask_hbm,
    innov_hbm,
    var_hbm,
    cols_hbm,
    r_out,
    info_out,
    c_out,
    s_out,
    q_out,
    p_out,
    x_out,
    norm,
    coef,
    x_v,
    col_ref,
    lev_ref,
    mask_ref,
    innov_ref,
    var_ref,
    cols_ref,
    xs,
    own,
    weights,
    w_side,
    c_own,
    ends_buf,
    near_buf,
    tail_buf,
    stat_buf,
    x_sem,
    in_sem,
    near_send,
    near_recv,
    head_send,
    head_recv,
    tail_send,
    tail_recv,
    stat_send,
    stat_recv,
):
    lat, lon = lax.axis_index("lat"), lax.axis_index("lon")
    bands, columns, width = x_v.shape
    obs = col_ref.shape[1]
    devices = lats * lons
    me = lat * lons + lon
    smalls = (
        (col_hbm, col_ref),
        (lev_hbm, lev_ref),
        (mask_hbm, mask_ref),
        (innov_hbm, innov_ref),
        (var_hbm, var_ref),
        (cols_hbm, cols_ref),
    )
    loads = [
        pltpu.make_async_copy(source, target, in_sem.at[i])
        for i, (source, target) in enumerate(smalls)
    ]
    x_loads = [pltpu.make_async_copy(x_hbm.at[b], x_v.at[b], x_sem.at[b]) for b in range(bands)]
    for load in loads + x_loads:
        load.start()
    barrier = pltpu.get_barrier_semaphore()
    near_buf[...] = jnp.zeros_like(near_buf)
    tail_buf[...] = jnp.zeros_like(tail_buf)

    for other in range(devices):

        @pl.when(me != other)
        def _():
            pl.semaphore_signal(
                barrier, inc=1, device_id=(other // lons, other % lons), device_id_type=MESH
            )

    xs[...] = jnp.zeros_like(xs)
    norm[...] = jnp.zeros_like(norm)
    pairs = width // LANES
    reach = RADIUS - 1
    ends = END_SLOTS
    first = lon * columns
    for load in loads:
        load.wait()
    mask = mask_ref[...].astype(F32)
    used_all = mask > 0.0
    local_int = jnp.where(used_all, col_ref[...] - first, -columns)
    local = local_int.astype(F32)
    lev = lev_ref[...]
    spot = (lax.shift_right_logical(lev, 1) * columns + col_ref[...] - first) * 2 + (lev & 1)
    scale = jnp.sqrt(mask / var_ref[...])
    params = jnp.concatenate([local, spot.astype(F32), scale, innov_ref[...]], axis=0)
    params = jnp.concatenate([params, jnp.zeros((LANES - 4 * bands, obs), F32)], axis=0)
    params = jnp.concatenate([params, jnp.zeros((LANES, LANES - obs), F32)], axis=1)
    upright = jnp.transpose(params)[:obs]
    earlier = iota((obs, obs), 0) < iota((obs, obs), 1)
    slot_ids = iota((ends, obs), 0)

    def stacked(kind):
        return jnp.concatenate(
            [upright[:, kind * bands + b : kind * bands + b + 1] for b in range(bands)], axis=0
        )

    marks = []
    for b in range(bands):
        row = local_int[b : b + 1]
        used = used_all[b : b + 1]
        same = (upright[:, b : b + 1] == local[b : b + 1]) & earlier
        rank = jnp.sum(jnp.where(same, 1.0, 0.0), axis=0, keepdims=True).astype(jnp.int32)
        bases = (row, row - (columns - reach), row + first - (cols_ref[b] - reach))
        mark = []
        for base in bases:
            fits = used & (base >= 0) & (base < reach)
            slot = jnp.where(fits, base * OC + rank, -1)
            mark.append(jnp.where(slot_ids == slot, 1.0, 0.0))
        marks.append(jnp.concatenate(mark, axis=0).astype(BF16))

    tapering = taper_weights(RADIUS)
    lane = iota((1, LANES), 1)
    lane_band, lane_col = lane // columns, lane % columns
    count = jnp.zeros((1, LANES), jnp.int32)
    for b in range(bands):
        count = jnp.where(lane_band == b, cols_ref[b], count)
    chooser = jnp.where(iota((LANES, LANES), 0) == lane_band, 1.0, 0.0).astype(BF16)
    source = dot(upright.astype(BF16), chooser).astype(jnp.int32)
    nth = iota((ends, LANES), 0) // OC

    def taper(place, limit):
        away = place - lane_col
        away = jnp.where(2 * away > limit, away - limit, away)
        away = jnp.where(2 * away < -limit, away + limit, away)
        away = jnp.abs(away)
        weight = jnp.zeros(place.shape, F32)
        for t in range(RADIUS):
            weight = jnp.where(away == t, tapering[t], weight)
        return weight.astype(BF16)

    near_own = taper(source, count)
    near_left = taper(nth - reach, FAR)
    near_right = taper(nth + columns, FAR)
    near_head = taper(nth + count - first, FAR)
    beside = (
        jnp.concatenate([near_right, near_head], axis=0),
        jnp.concatenate([near_left, near_head], axis=0),
    )
    weights[0] = jnp.concatenate([near_own, beside[0]], axis=0)
    weights[1] = jnp.concatenate([near_own, beside[1]], axis=0)

    spots = stacked(1).astype(jnp.int32)
    scales = stacked(2)
    depth = pairs * columns
    gathered = []
    for b in range(bands):
        index = lax.shift_right_logical(spots[b * obs : (b + 1) * obs], 1)
        onehot = jnp.where(iota((obs, depth), 1) == index, 1.0, 0.0).astype(BF16)
        x_loads[b].wait()
        field = jnp.concatenate(
            [x_v[b, :, p * LANES : (p + 1) * LANES] for p in range(pairs)], axis=0
        )
        gathered.append(dot(onehot, field))
    found = jnp.concatenate(gathered, axis=0)
    total = bands * obs
    low_t = iota((total, LANES), 1) < K
    even = (spots & 1) == 0
    picked = jnp.where(low_t == even, found, pltpu.roll(found, K, 1))
    anomaly = picked - jnp.mean(picked, axis=1, keepdims=True)
    departs = (scales * (anomaly - stacked(3))).astype(BF16)
    wide = departs.astype(F32)
    own[...] = wide
    centre = jnp.mean(wide, axis=1, keepdims=True)
    spread = wide - centre
    numerator = jnp.sum(centre * centre, axis=0, keepdims=True)
    spread_row = jnp.sum(spread * spread, axis=0, keepdims=True)
    mask_row = jnp.sum(mask, axis=0, keepdims=True)
    denominator = jnp.sum(spread_row, axis=1, keepdims=True) * (0.5 / (K - 1)) + jnp.sum(
        mask_row, axis=1, keepdims=True
    )
    stat_buf[me] = jnp.where(iota((1, LANES), 1) == 0, numerator, denominator)

    low = iota((obs, LANES), 1) < K
    for q in range(bands // PAIR):
        mark = jnp.concatenate([marks[2 * q], marks[2 * q + 1]], axis=1)
        one = wide[(2 * q) * obs : (2 * q + 1) * obs]
        two = wide[(2 * q + 1) * obs : (2 * q + 2) * obs]
        both = jnp.concatenate(
            [jnp.where(low, one, 0.0), jnp.where(low, 0.0, two)], axis=0
        ).astype(BF16)
        compact = dot(mark, both).astype(BF16)
        for kind in range(3):
            ends_buf[kind, q] = compact[kind * ends : (kind + 1) * ends]

    rows_x = xs.shape[0] // columns
    groups = columns // GROUP
    low_x = iota((rows_x, LANES), 1) < K
    def spread_band(b, carry):
        for p in range(pairs):
            strip = x_v[b, :, p * LANES : (p + 1) * LANES].astype(F32)
            xs[pl.ds(p, columns, stride=rows_x), :] = strip
        for g in range(groups):
            halves = []
            for c in (g * GROUP, g * GROUP + 2):
                here = xs[c * rows_x : (c + 1) * rows_x, :]
                there = xs[(c + 1) * rows_x : (c + 2) * rows_x, :]
                halves.append(
                    jnp.concatenate(
                        [
                            jnp.where(low_x, here, pltpu.roll(there, K, 1)),
                            jnp.where(low_x, pltpu.roll(here, K, 1), there),
                        ],
                        axis=0,
                    ).astype(BF16)
                )
            x_out[b * groups + g] = jnp.concatenate(halves, axis=1)
        return carry

    eye = jnp.where(iota((K, SPAN), 0) == iota((K, SPAN), 1) % K, 1.0, 0.0)
    spare = pairs
    expand_row = iota((LANES, SPAN), 0) - iota((LANES, SPAN), 1) // K
    row_id = iota((16, SPAN), 0) + 16

    edge = -(-reach // GROUP)

    def half_gram(slot):
        spread = slot - jnp.mean(slot, axis=1, keepdims=True)
        rows = slot.shape[0]
        square = jnp.concatenate([slot, jnp.zeros((LANES - rows, LANES), F32)], axis=0)
        turned = jnp.transpose(square)[:K, :rows]
        centre = jnp.mean(turned, axis=0, keepdims=True)
        left = jnp.concatenate([turned - centre, -centre, jnp.zeros((15, rows), F32)], axis=0)
        return left.astype(BF16), spread

    def weighted(spread, wide_w):
        return jnp.concatenate(
            [
                (spread * wide_w[:, :LANES]).astype(BF16),
                (spread * wide_w[:, LANES:]).astype(BF16),
            ],
            axis=1,
        )

    def own_part(p, carry):
        made = []
        for j in range(PAIR):
            start = pl.multiple_of((p * PAIR + j) * obs, obs)
            made.append(half_gram(own[pl.ds(start, obs), :]))

        def column_group(j, g):
            i = (p * PAIR + j) * groups + g
            picker = jnp.where(
                expand_row == (p * PAIR + j) * columns + g * GROUP, 1.0, 0.0
            ).astype(BF16)
            wide_w = dot(weights[1 if g < edge else 0], picker)
            yield
            w_side[i] = wide_w[obs:]
            gram = dot(made[j][0], weighted(made[j][1], wide_w[:obs]))
            yield
            c_own[i] = gram

        wavefront([column_group(j, g) for j in range(PAIR) for g in range(groups)], GAP_OWN)
        return carry

    soon = lon < lons // 2
    bands_before = jnp.where(soon, bands, 0)
    pairs_before = jnp.where(soon, bands // PAIR, 0)
    lax.fori_loop(0, bands_before, spread_band, 0)
    lax.fori_loop(0, pairs_before, own_part, 0)

    pl.semaphore_wait(barrier, devices - 1)

    def stat_copy(slot, size, other):
        return pltpu.make_async_remote_copy(
            src_ref=stat_buf.at[pl.ds(slot, size)],
            dst_ref=stat_buf.at[pl.ds(slot, size)],
            send_sem=stat_send,
            recv_sem=stat_recv,
            device_id=(other // lons, other % lons),
            device_id_type=MESH,
        )

    def near_copy(kind, slot, other):
        return pltpu.make_async_remote_copy(
            src_ref=ends_buf.at[kind],
            dst_ref=near_buf.at[slot],
            send_sem=near_send.at[slot],
            recv_sem=near_recv.at[slot],
            device_id=(lat, other),
            device_id_type=MESH,
        )

    def head_copy(other):
        return pltpu.make_async_remote_copy(
            src_ref=ends_buf.at[0],
            dst_ref=near_buf.at[2],
            send_sem=head_send.at[other],
            recv_sem=head_recv,
            device_id=(lat, other),
            device_id_type=MESH,
        )

    def tail_copy(slot):
        return pltpu.make_async_remote_copy(
            src_ref=ends_buf.at[2],
            dst_ref=tail_buf.at[slot],
            send_sem=tail_send,
            recv_sem=tail_recv,
            device_id=(lat, 0),
            device_id_type=MESH,
        )

    @pl.when(lon < lons - 1)
    def _():
        near_copy(1, 0, lon + 1).start()

    @pl.when(lon > 0)
    def _():
        near_copy(0, 1, lon - 1).start()
        tail_copy(lon).start()

    @pl.when(lon == 0)
    def _():
        for other in range(lons - 1, 0, -1):
            head_copy(other).start()

    for other in range(devices):

        @pl.when(me != other)
        def _():
            stat_copy(me, 1, other).start()

    lax.fori_loop(bands_before, bands, spread_band, 0)
    lax.fori_loop(pairs_before, bands // PAIR, own_part, 0)

    def early(chosen, extras, block, offset):
        made = []
        low_e = iota(extras[0].shape, 1) < K
        skip = 2 * ends - extras[0].shape[0]
        for extra in extras:
            swapped = pltpu.roll(extra, K, 1)
            made.append(half_gram(jnp.where(low_e, extra, swapped)))
            made.append(half_gram(jnp.where(low_e, swapped, extra)))
        places = [(j, j * groups + g) for j in range(bands) for g in chosen]

        def column_group(line, j, i):
            gram = c_own[i] + dot(made[j][0], weighted(made[j][1], w_side[i, skip:]))
            yield
            c = gram[:K]
            c_out[i] = c
            narrow = c.astype(BF16)
            mean = gram[K : K + 1]
            old = x_out[i]
            middle = jnp.where(row_id == spare, mean, old[16:32].astype(F32)).astype(BF16)
            field = jnp.concatenate([old[:16], middle, old[32:]], axis=0)
            x_out[i] = field
            norm[block, 0, line : line + 1, :] = jnp.sum(c * c, axis=0, keepdims=True)
            norm[block, 1, line : line + 1, :] = jnp.sum(c * eye, axis=0, keepdims=True)
            both = dot(jnp.concatenate([narrow, field], axis=0), block_diag(narrow))
            yield
            s_out[i] = both[:K]
            p_out[i] = both[K:]
            cube = dot(narrow, block_diag(both[:K].astype(BF16)))
            yield
            q_out[i] = cube

        return [column_group(offset + n, j, i) for n, (j, i) in enumerate(places)]

    @pl.when(lon > 0)
    def _():
        head_copy(lon).wait_recv()

    halves = bands // PAIR
    centre_groups = range(edge, groups - edge)
    heads = [near_buf[2, p].astype(F32) for p in range(halves)]
    wavefront(early(centre_groups, heads, 0, 0), GAP_EARLY)

    everyone = stat_copy(0, devices - 1, 0)
    everyone.wait_send()
    everyone.wait_recv()
    stats = jnp.sum(stat_buf[...], axis=0)
    inflation = (stats[:, 0:1] + 1e-06) / stats[:, 1:2]
    shift = (K - 1) / inflation
    line = iota((8, LANES), 0)
    info = jnp.zeros((8, LANES), F32)
    for b in range(bands):
        info = jnp.where(line == b, (cols_ref[b] - first).astype(F32), info)
    info_out[...] = info
    ones_bd = block_diag(jnp.ones((K, SPAN), BF16))

    def settle(block):
        squares = norm[block, 0] + shift * (2.0 * norm[block, 1] + shift)
        coarse = squares.astype(BF16)
        fine = (squares - coarse.astype(F32)).astype(BF16)
        sums = dot(jnp.concatenate([coarse, fine], axis=0), ones_bd)
        size = squares.shape[0]
        inv = lax.rsqrt(sums[:size] + sums[size:])
        scaling = jnp.sqrt((K - 1.0) * inv)
        beta = 1.0 - shift * inv
        beta1 = beta * beta * (0.75 + 0.25 * beta)
        beta2 = beta1 * beta1 * (0.75 + 0.25 * beta1)
        a0 = 1.0 + 0.5 * beta
        a1 = 1.0 + 0.5 * beta1
        half1 = 0.5 / a1
        c0 = (1.0 + 0.5 * beta2) * (1.0 + (0.375 + 0.125 * beta2) * beta2 * beta2)
        c1 = 0.5 + beta2 * (0.75 + beta2 * (0.9375 + 0.25 * beta2))
        c2 = 0.375 + beta2 * (0.9375 + 0.375 * beta2)
        c3 = 0.3125 + 0.25 * beta2
        up, down = c1 / c0, c0 / c1
        whole = a0 * a1 * c0
        table = (
            -inv * (1.5 * beta + 0.75 * beta * beta) * half1,
            inv * inv * (0.75 + 0.75 * beta) * half1,
            -0.25 * inv * inv * inv * half1,
            -0.5 * inv / a0,
            2.0 * a1 * up * (1.5 * beta1 + 0.75 * beta1 * beta1),
            4.0 * a1 * a1 * up * (0.75 + 0.75 * beta1),
            2.0 * a1 * a1 * a1 * up,
            c2 / c0 * down * down,
            c3 / c0 * down * down * down,
            0.0625 / c0 * (down * down) * (down * down),
            whole * whole * inv,
            (1.0 - scaling * whole) * (1.0 / K),
            scaling * whole,
        )
        for t, value in enumerate(table):
            coef[block, t] = value

    def finish(work):
        def k(t, w):
            return coef[w[0], t, w[1] : w[1] + 1, :]

        def wide_x(w):
            return x_out[w[2]].astype(F32)

        held = {}

        def column_group(n, w):
            i = w[2]
            m = k(0, w) * c_out[i] + k(1, w) * s_out[i] + k(2, w) * q_out[i]
            x = wide_x(w) + k(3, w) * p_out[i]
            m_b = m.astype(BF16)
            both = dot(jnp.concatenate([m_b, x.astype(BF16)], axis=0), block_diag(m_b))
            yield
            square = both[:K]
            cube = dot(m_b, block_diag(square.astype(BF16)))
            x = x + both[K:]
            yield
            m_b = (k(4, w) * m + k(5, w) * square + k(6, w) * cube).astype(BF16)
            x_b = x.astype(BF16)
            both = dot(jnp.concatenate([m_b, x_b], axis=0), block_diag(m_b))
            yield
            fixed = block_diag(both[:K].astype(BF16))
            quad = dot(x_b, fixed)
            part = k(7, w) * x + k(8, w) * both[K:]
            x = x + both[K:]
            yield
            last = dot((part + k(9, w) * quad).astype(BF16), fixed)
            yield
            x = x + last
            step = x[spare : spare + 1] * k(10, w)
            held[n] = (x * step + wide_x(w) * k(11, w)).astype(BF16)
            if n % SHARED == SHARED - 1 or n + 1 == len(work):
                first_n = n - n % SHARED
                stack = jnp.concatenate([held[v] for v in range(first_n, n + 1)], axis=0)
                means = dot(stack, ones_bd)
                rows = stack.shape[0] // (n + 1 - first_n)
                for v in range(first_n, n + 1):
                    held[v] = means[(v - first_n) * rows : (v - first_n + 1) * rows]
            yield
            yield
            r_out[i] = k(12, w) * x + held[n]

        return [column_group(n, w) for n, w in enumerate(work)]

    def lines(block, offset, chosen):
        places = [b * groups + g for b in range(bands) for g in chosen]
        return [(block, offset + n, i) for n, i in enumerate(places)]

    settle(0)
    wavefront(finish(lines(0, 0, centre_groups)), GAP_LATE)

    @pl.when(lon < lons - 1)
    def _():
        near_copy(0, 1, lon + 1).wait_recv()

    @pl.when(lon > 0)
    def _():
        near_copy(1, 0, lon - 1).wait_recv()

    @pl.when(lon == 0)
    def _():
        pltpu.make_async_remote_copy(
            src_ref=tail_buf.at[pl.ds(1, lons - 1)],
            dst_ref=tail_buf.at[pl.ds(1, lons - 1)],
            send_sem=tail_send,
            recv_sem=tail_recv,
            device_id=(lat, 0),
            device_id_type=MESH,
        ).wait_recv()

    lefts, rights = [], []
    for p in range(halves):
        ahead = near_buf[0, p].astype(F32)
        for other in range(1, lons):
            ahead = ahead + tail_buf[other, p].astype(F32)
        lefts.append(jnp.concatenate([ahead, heads[p]], axis=0))
        rights.append(jnp.concatenate([near_buf[1, p].astype(F32), heads[p]], axis=0))
    left_groups, right_groups = range(edge), range(groups - edge, groups)
    wavefront(
        early(right_groups, rights, 1, 0) + early(left_groups, lefts, 1, bands * edge), GAP_EARLY
    )
    settle(1)
    wavefront(
        finish(lines(1, 0, right_groups) + lines(1, bands * edge, left_groups)), GAP_LATE
    )

    @pl.when(lon > 0)
    def _():
        tail_copy(lon).wait_send()
        near_copy(0, 1, lon - 1).wait_send()

    @pl.when(lon == 0)
    def _():
        for other in range(1, lons):
            head_copy(other).wait_send()

    @pl.when(lon < lons - 1)
    def _():
        near_copy(1, 0, lon + 1).wait_send()


def layout_kernel(r_ref, info_ref, out_hbm, ys, obuf, out_sem):
    bands, columns, width = obuf.shape
    pairs = width // LANES
    groups = columns // GROUP
    rows_x = ys.shape[1] // columns
    low_x = iota((rows_x, LANES), 1) < K

    def write(b):
        return pltpu.make_async_copy(obuf.at[b], out_hbm.at[b], out_sem.at[b])

    for b in range(bands):
        slot = b % PAIR
        for g in range(groups):
            result = r_ref[b * groups + g]
            for side in range(2):
                c = g * GROUP + 2 * side
                got = result[:, side * LANES : (side + 1) * LANES]
                even, odd = got[:rows_x], got[rows_x:]
                ys[slot, c * rows_x : (c + 1) * rows_x, :] = jnp.where(
                    low_x, even, pltpu.roll(odd, K, 1)
                )
                ys[slot, (c + 1) * rows_x : (c + 2) * rows_x, :] = jnp.where(
                    low_x, pltpu.roll(even, K, 1), odd
                )
        keep = iota((columns, LANES), 0).astype(F32) < info_ref[b : b + 1, :]
        for t in range(pairs):
            obuf[b, :, t * LANES : (t + 1) * LANES] = jnp.where(
                keep, ys[slot, pl.ds(t, columns, stride=rows_x), :], 0.0
            ).astype(BF16)
        write(b).start()
    for b in range(bands):
        write(b).wait()


def per_device(lats, lons, background, band_cols, obs_col, obs_lev, obs_mask, innov, obs_var):
    bands, columns, width = background.shape
    obs = obs_col.shape[1]
    pairs = width // LANES
    devices = lats * lons
    vmem = pl.BlockSpec(memory_space=pltpu.VMEM)
    hbm = pl.BlockSpec(memory_space=pltpu.HBM)
    dma = pltpu.SemaphoreType.DMA
    rows_x = -(-(pairs + 1) // 8) * 8
    halves = bands // PAIR
    slots = obs + 2 * END_SLOTS
    total = bands * columns // GROUP
    rim = 2 * -(-(RADIUS - 1) // GROUP) * bands
    most = -(-max(rim, total - rim) // 8) * 8
    room = 16 * 1024 * 1024
    arrays = (background, obs_col, obs_lev, obs_mask, innov, obs_var, band_cols)
    groups_f32 = pltpu.VMEM((total, K, SPAN), F32)
    result, info = pl.pallas_call(
        functools.partial(exchange_kernel, lats, lons),
        out_shape=(
            jax.ShapeDtypeStruct((total, 2 * rows_x, SPAN), F32),
            jax.ShapeDtypeStruct((8, LANES), F32),
        ),
        in_specs=[hbm] * 7,
        out_specs=(vmem,) * 2,
        scratch_shapes=[
            groups_f32,
            groups_f32,
            groups_f32,
            pltpu.VMEM((total, 2 * rows_x, SPAN), F32),
            pltpu.VMEM((total, 2 * rows_x, SPAN), BF16),
            pltpu.VMEM((2, 2, most, SPAN), F32),
            pltpu.VMEM((2, 13, most, SPAN), F32),
            pltpu.VMEM((bands, columns, width), BF16),
            pltpu.VMEM((bands, obs), jnp.int32),
            pltpu.VMEM((bands, obs), jnp.int32),
            pltpu.VMEM((bands, obs), jnp.int32),
            pltpu.VMEM((bands, obs), F32),
            pltpu.VMEM((bands, obs), F32),
            pltpu.SMEM((bands,), jnp.int32),
            pltpu.VMEM((columns * rows_x, LANES), F32),
            pltpu.VMEM((bands * obs, LANES), F32),
            pltpu.VMEM((2, slots, LANES), BF16),
            pltpu.VMEM((total, 2 * END_SLOTS, SPAN), F32),
            pltpu.VMEM((total, K + 16, SPAN), F32),
            pltpu.VMEM((3, halves, END_SLOTS, LANES), BF16),
            pltpu.VMEM((3, halves, END_SLOTS, LANES), BF16),
            pltpu.VMEM((lons, halves, END_SLOTS, LANES), BF16),
            pltpu.VMEM((devices, 1, LANES), F32),
            dma((bands,)),
            dma((6,)),
            dma((2,)),
            dma((2,)),
            dma((lons,)),
            dma,
            dma,
            dma,
            dma,
            dma,
        ],
        compiler_params=pltpu.CompilerParams(
            collective_id=0, has_side_effects=True, vmem_limit_bytes=2 * room
        ),
        name="exchange",
    )(*(pltpu.with_memory_space_constraint(a, pltpu.HBM) for a in arrays))
    return pl.pallas_call(
        layout_kernel,
        out_shape=jax.ShapeDtypeStruct(background.shape, BF16),
        in_specs=[vmem] * 2,
        out_specs=hbm,
        scratch_shapes=[
            pltpu.VMEM((PAIR, columns * rows_x, LANES), F32),
            pltpu.VMEM((bands, columns, width), BF16),
            dma((bands,)),
        ],
        compiler_params=pltpu.CompilerParams(vmem_limit_bytes=room),
        name="layout",
    )(result, info)


def solution(mesh):
    placed = (P("lat", "lon", None), P("lat")) + (P("lat", "lon"),) * 5
    return jax.shard_map(
        functools.partial(per_device, mesh.shape["lat"], mesh.shape["lon"]),
        mesh=mesh,
        in_specs=placed,
        out_specs=P("lat", "lon", None),
        check_vma=False,
    )
```

time: 20.8 us -> 18.3 us (0.88)
  Pallas kernels: 20.6 us -> 18.1 us
    pallas_call x1, Pallas kernels: 5.94 us -> 1.25 us  [per_device(): pl.pallas_call(layout_kernel, out_shape=jax.ShapeDtypeStruct(background.s...]
    pallas_call x1, Pallas kernels: 14.7 us -> 16.9 us  [per_device(): pl.pallas_call(functools.partial(exchange_kernel, lats, lons), out_shape=...]
where the time goes in v3:
time: 18.3 us; the launch traced here: 18.1 us
  Pallas kernels  18.1 us (99%)
    pallas_call x1, Pallas kernels, per_device(): pl.pallas_call(functools.partial(exchange_kernel, lats, lons), out_shape=...  16.9 us
    pallas_call x1, Pallas kernels, per_device(): pl.pallas_call(layout_kernel, out_shape=jax.ShapeDtypeStruct(background.s...  1.25 us

profile of v3, /device:TPU:0, one launch (start us, length us, event | category | flops | bytes accessed | tf_op | source)
XLA Modules:
  0.0 18.1 jit_solution(11331312357263821918)
XLA Ops:
  0.0 16.9 %exchange.1 = (f32[32,48,256]{2,1,0:T(8,128)S(1)}, f32[8,128]{1,0:T(8,128)S(1)}) custom-call(bf16[4,32,2560]{2,1,0:T(8,128)(2,1)} %x_hbm.1, s32[4,64]{1,0:T(4,128)} %col_hbm.1, s32[4,64]{1,0:T(4,128)} %lev_hbm.1, s32[4,64]{1,0:T(4,128)} %mask_hbm.1, f32[4,64]{1,0:T(4,128)} %innov_hbm.1, f32[4,64]{1,0:T(4,128)} %var_hbm.1, s32[4]{0:T(128)} %cols_hbm.1), custom_call_target="tpu_custom_call" | custom-call | tf_op jit(solution)/shard_map/exchange/pallas_call | solution.py:673
  16.9 1.2 %layout.1 = bf16[4,32,2560]{2,1,0:T(8,128)(2,1)} custom-call(f32[32,48,256]{2,1,0:T(8,128)S(1)} %get-tuple-element.7.r_ref, f32[8,128]{1,0:T(8,128)S(1)} %get-tuple-element.8.info_ref), custom_call_target="tpu_custom_call" | custom-call | tf_op jit(solution)/shard_map/layout/pallas_call | solution.py:721

commit v4 on v3

--- a/solution.py
+++ b/solution.py
@@ -269,17 +269,21 @@
     )
     stat_buf[me] = jnp.where(iota((1, LANES), 1) == 0, numerator, denominator)
 
-    low = iota((obs, LANES), 1) < K
-    for q in range(bands // PAIR):
-        mark = jnp.concatenate([marks[2 * q], marks[2 * q + 1]], axis=1)
-        one = wide[(2 * q) * obs : (2 * q + 1) * obs]
-        two = wide[(2 * q + 1) * obs : (2 * q + 2) * obs]
-        both = jnp.concatenate(
-            [jnp.where(low, one, 0.0), jnp.where(low, 0.0, two)], axis=0
-        ).astype(BF16)
-        compact = dot(mark, both).astype(BF16)
-        for kind in range(3):
-            ends_buf[kind, q] = compact[kind * ends : (kind + 1) * ends]
+    def compact_ends():
+        low = iota((obs, LANES), 1) < K
+        for q in range(bands // PAIR):
+            mark = jnp.concatenate([marks[2 * q], marks[2 * q + 1]], axis=1)
+            one = wide[(2 * q) * obs : (2 * q + 1) * obs]
+            two = wide[(2 * q + 1) * obs : (2 * q + 2) * obs]
+            both = jnp.concatenate(
+                [jnp.where(low, one, 0.0), jnp.where(low, 0.0, two)], axis=0
+            ).astype(BF16)
+            compact = dot(mark, both).astype(BF16)
+            for kind in range(3):
+                ends_buf[kind, q] = compact[kind * ends : (kind + 1) * ends]
+
+    soon = lon < lons // 2
+    pl.when(soon)(compact_ends)
 
     rows_x = xs.shape[0] // columns
     groups = columns // GROUP
@@ -351,7 +355,6 @@
         wavefront([column_group(j, g) for j in range(PAIR) for g in range(groups)], GAP_OWN)
         return carry
 
-    soon = lon < lons // 2
     bands_before = jnp.where(soon, bands, 0)
     pairs_before = jnp.where(soon, bands // PAIR, 0)
     lax.fori_loop(0, bands_before, spread_band, 0)
@@ -399,15 +402,6 @@
             device_id_type=MESH,
         )
 
-    @pl.when(lon < lons - 1)
-    def _():
-        near_copy(1, 0, lon + 1).start()
-
-    @pl.when(lon > 0)
-    def _():
-        near_copy(0, 1, lon - 1).start()
-        tail_copy(lon).start()
-
     @pl.when(lon == 0)
     def _():
         for other in range(lons - 1, 0, -1):
@@ -418,6 +412,17 @@
         @pl.when(me != other)
         def _():
             stat_copy(me, 1, other).start()
+
+    pl.when(jnp.logical_not(soon))(compact_ends)
+
+    @pl.when(lon < lons - 1)
+    def _():
+        near_copy(1, 0, lon + 1).start()
+
+    @pl.when(lon > 0)
+    def _():
+        near_copy(0, 1, lon - 1).start()
+        tail_copy(lon).start()
 
     lax.fori_loop(bands_before, bands, spread_band, 0)
     lax.fori_loop(pairs_before, bands // PAIR, own_part, 0)
@@ -464,26 +469,8 @@
     heads = [near_buf[2, p].astype(F32) for p in range(halves)]
     wavefront(early(centre_groups, heads, 0, 0), GAP_EARLY)
 
-    everyone = stat_copy(0, devices - 1, 0)
-    everyone.wait_send()
-    everyone.wait_recv()
-    stats = jnp.sum(stat_buf[...], axis=0)
-    inflation = (stats[:, 0:1] + 1e-06) / stats[:, 1:2]
-    shift = (K - 1) / inflation
-    line = iota((8, LANES), 0)
-    info = jnp.zeros((8, LANES), F32)
-    for b in range(bands):
-        info = jnp.where(line == b, (cols_ref[b] - first).astype(F32), info)
-    info_out[...] = info
-    ones_bd = block_diag(jnp.ones((K, SPAN), BF16))
-
-    def settle(block):
-        squares = norm[block, 0] + shift * (2.0 * norm[block, 1] + shift)
-        coarse = squares.astype(BF16)
-        fine = (squares - coarse.astype(F32)).astype(BF16)
-        sums = dot(jnp.concatenate([coarse, fine], axis=0), ones_bd)
-        size = squares.shape[0]
-        inv = lax.rsqrt(sums[:size] + sums[size:])
+    def settle(block, shift, sums):
+        inv = lax.rsqrt(sums[0] + shift * (2.0 * sums[1] + K * shift))
         scaling = jnp.sqrt((K - 1.0) * inv)
         beta = 1.0 - shift * inv
         beta1 = beta * beta * (0.75 + 0.25 * beta)
@@ -558,7 +545,18 @@
                     held[v] = means[(v - first_n) * rows : (v - first_n + 1) * rows]
             yield
             yield
-            r_out[i] = k(12, w) * x + held[n]
+            result = k(12, w) * x + held[n]
+            b, g = i // groups, i % groups
+            for side in range(2):
+                c = g * GROUP + 2 * side
+                got = result[:, side * LANES : (side + 1) * LANES]
+                evens, odds = got[:rows_x], got[rows_x:]
+                r_out[b, c * rows_x : (c + 1) * rows_x, :] = jnp.where(
+                    low_x, evens, pltpu.roll(odds, K, 1)
+                )
+                r_out[b, (c + 1) * rows_x : (c + 2) * rows_x, :] = jnp.where(
+                    low_x, pltpu.roll(evens, K, 1), odds
+                )
 
         return [column_group(n, w) for n, w in enumerate(work)]
 
@@ -566,7 +564,30 @@
         places = [b * groups + g for b in range(bands) for g in chosen]
         return [(block, offset + n, i) for n, i in enumerate(places)]
 
-    settle(0)
+    ones_bd = block_diag(jnp.ones((K, SPAN), BF16))
+
+    def block_sums(block):
+        both = jnp.concatenate([norm[block, 0], norm[block, 1]], axis=0)
+        coarse = both.astype(BF16)
+        fine = (both - coarse.astype(F32)).astype(BF16)
+        size = both.shape[0]
+        sums = dot(jnp.concatenate([coarse, fine], axis=0), ones_bd)
+        sums = sums[:size] + sums[size:]
+        return sums[: size // 2], sums[size // 2 :]
+
+    first_sums = block_sums(0)
+    everyone = stat_copy(0, devices - 1, 0)
+    everyone.wait_send()
+    everyone.wait_recv()
+    stats = jnp.sum(stat_buf[...], axis=0)
+    inflation = (stats[:, 0:1] + 1e-06) / stats[:, 1:2]
+    shift = (K - 1) / inflation
+    line = iota((8, LANES), 0)
+    info = jnp.zeros((8, LANES), F32)
+    for b in range(bands):
+        info = jnp.where(line == b, (cols_ref[b] - first).astype(F32), info)
+    info_out[...] = info
+    settle(0, shift, first_sums)
     wavefront(finish(lines(0, 0, centre_groups)), GAP_LATE)
 
     @pl.when(lon < lons - 1)
@@ -599,7 +620,7 @@
     wavefront(
         early(right_groups, rights, 1, 0) + early(left_groups, lefts, 1, bands * edge), GAP_EARLY
     )
-    settle(1)
+    settle(1, shift, block_sums(1))
     wavefront(
         finish(lines(1, 0, right_groups) + lines(1, bands * edge, left_groups)), GAP_LATE
     )
@@ -619,34 +640,19 @@
         near_copy(1, 0, lon + 1).wait_send()
 
 
-def layout_kernel(r_ref, info_ref, out_hbm, ys, obuf, out_sem):
+def layout_kernel(r_ref, info_ref, out_hbm, obuf, out_sem):
     bands, columns, width = obuf.shape
     pairs = width // LANES
-    groups = columns // GROUP
-    rows_x = ys.shape[1] // columns
-    low_x = iota((rows_x, LANES), 1) < K
+    rows_x = r_ref.shape[1] // columns
 
     def write(b):
         return pltpu.make_async_copy(obuf.at[b], out_hbm.at[b], out_sem.at[b])
 
     for b in range(bands):
-        slot = b % PAIR
-        for g in range(groups):
-            result = r_ref[b * groups + g]
-            for side in range(2):
-                c = g * GROUP + 2 * side
-                got = result[:, side * LANES : (side + 1) * LANES]
-                even, odd = got[:rows_x], got[rows_x:]
-                ys[slot, c * rows_x : (c + 1) * rows_x, :] = jnp.where(
-                    low_x, even, pltpu.roll(odd, K, 1)
-                )
-                ys[slot, (c + 1) * rows_x : (c + 2) * rows_x, :] = jnp.where(
-                    low_x, pltpu.roll(even, K, 1), odd
-                )
         keep = iota((columns, LANES), 0).astype(F32) < info_ref[b : b + 1, :]
         for t in range(pairs):
             obuf[b, :, t * LANES : (t + 1) * LANES] = jnp.where(
-                keep, ys[slot, pl.ds(t, columns, stride=rows_x), :], 0.0
+                keep, r_ref[b, pl.ds(t, columns, stride=rows_x), :], 0.0
             ).astype(BF16)
         write(b).start()
     for b in range(bands):
@@ -673,7 +679,7 @@
     result, info = pl.pallas_call(
         functools.partial(exchange_kernel, lats, lons),
         out_shape=(
-            jax.ShapeDtypeStruct((total, 2 * rows_x, SPAN), F32),
+            jax.ShapeDtypeStruct((bands, columns * rows_x, LANES), F32),
             jax.ShapeDtypeStruct((8, LANES), F32),
         ),
         in_specs=[hbm] * 7,
@@ -724,7 +730,6 @@
         in_specs=[vmem] * 2,
         out_specs=hbm,
         scratch_shapes=[
-            pltpu.VMEM((PAIR, columns * rows_x, LANES), F32),
             pltpu.VMEM((bands, columns, width), BF16),
             dma((bands,)),
         ],

time: 18.3 us -> 17.9 us (0.978)
  Pallas kernels: 18.1 us -> 17.7 us
    pallas_call x1, Pallas kernels: 1.25 us -> 1 us  [per_device(): pl.pallas_call(layout_kernel, out_shape=jax.ShapeDtypeStruct(background.s...]
where the time goes in v4:
time: 17.9 us; the launch traced here: 17.7 us
  Pallas kernels  17.7 us (99%)
    pallas_call x1, Pallas kernels, per_device(): pl.pallas_call(functools.partial(exchange_kernel, lats, lons), out_shape=...  16.7 us
    pallas_call x1, Pallas kernels, per_device(): pl.pallas_call(layout_kernel, out_shape=jax.ShapeDtypeStruct(background.s...  1 us

profile of v4, /device:TPU:0, one launch (start us, length us, event | category | flops | bytes accessed | tf_op | source)
XLA Modules:
  0.0 17.7 jit_solution(16616972958543574548)
XLA Ops:
  0.0 16.7 %exchange.1 = (f32[4,768,128]{2,1,0:T(8,128)S(1)}, f32[8,128]{1,0:T(8,128)S(1)}) custom-call(bf16[4,32,2560]{2,1,0:T(8,128)(2,1)} %x_hbm.1, s32[4,64]{1,0:T(4,128)} %col_hbm.1, s32[4,64]{1,0:T(4,128)} %lev_hbm.1, s32[4,64]{1,0:T(4,128)} %mask_hbm.1, f32[4,64]{1,0:T(4,128)} %innov_hbm.1, f32[4,64]{1,0:T(4,128)} %var_hbm.1, s32[4]{0:T(128)} %cols_hbm.1), custom_call_target="tpu_custom_call" | custom-call | tf_op jit(solution)/shard_map/exchange/pallas_call | solution.py:679
  16.7 1.0 %layout.1 = bf16[4,32,2560]{2,1,0:T(8,128)(2,1)} custom-call(f32[4,768,128]{2,1,0:T(8,128)S(1)} %get-tuple-element.7.r_ref, f32[8,128]{1,0:T(8,128)S(1)} %get-tuple-element.8.info_ref), custom_call_target="tpu_custom_call" | custom-call | tf_op jit(solution)/shard_map/layout/pallas_call | solution.py:727

commit v5 on v4

--- a/solution.py
+++ b/solution.py
@@ -404,7 +404,7 @@
 
     @pl.when(lon == 0)
     def _():
-        for other in range(lons - 1, 0, -1):
+        for other in [*range(2, lons), 1]:
             head_copy(other).start()
 
     for other in range(devices):
@@ -468,6 +468,16 @@
     centre_groups = range(edge, groups - edge)
     heads = [near_buf[2, p].astype(F32) for p in range(halves)]
     wavefront(early(centre_groups, heads, 0, 0), GAP_EARLY)
+
+    @pl.when(lon < lons - 1)
+    def _():
+        near_copy(0, 1, lon + 1).wait_recv()
+
+    rights = [
+        jnp.concatenate([near_buf[1, p].astype(F32), heads[p]], axis=0) for p in range(halves)
+    ]
+    left_groups, right_groups = range(edge), range(groups - edge, groups)
+    wavefront(early(right_groups, rights, 1, 0), GAP_EARLY)
 
     def settle(block, shift, sums):
         inv = lax.rsqrt(sums[0] + shift * (2.0 * sums[1] + K * shift))
@@ -590,10 +600,6 @@
     settle(0, shift, first_sums)
     wavefront(finish(lines(0, 0, centre_groups)), GAP_LATE)
 
-    @pl.when(lon < lons - 1)
-    def _():
-        near_copy(0, 1, lon + 1).wait_recv()
-
     @pl.when(lon > 0)
     def _():
         near_copy(1, 0, lon - 1).wait_recv()
@@ -609,17 +615,13 @@
             device_id_type=MESH,
         ).wait_recv()
 
-    lefts, rights = [], []
+    lefts = []
     for p in range(halves):
         ahead = near_buf[0, p].astype(F32)
         for other in range(1, lons):
             ahead = ahead + tail_buf[other, p].astype(F32)
         lefts.append(jnp.concatenate([ahead, heads[p]], axis=0))
-        rights.append(jnp.concatenate([near_buf[1, p].astype(F32), heads[p]], axis=0))
-    left_groups, right_groups = range(edge), range(groups - edge, groups)
-    wavefront(
-        early(right_groups, rights, 1, 0) + early(left_groups, lefts, 1, bands * edge), GAP_EARLY
-    )
+    wavefront(early(left_groups, lefts, 1, bands * edge), GAP_EARLY)
     settle(1, shift, block_sums(1))
     wavefront(
         finish(lines(1, 0, right_groups) + lines(1, bands * edge, left_groups)), GAP_LATE

time: 17.9 us -> 17.7 us (0.989)
  Pallas kernels: 17.7 us -> 17.5 us
    pallas_call x1, Pallas kernels: 16.7 us -> 16.5 us  [per_device(): pl.pallas_call(functools.partial(exchange_kernel, lats, lons), out_shape=...]
where the time goes in v5:
time: 17.7 us; the launch traced here: 17.5 us
  Pallas kernels  17.5 us (99%)
    pallas_call x1, Pallas kernels, per_device(): pl.pallas_call(functools.partial(exchange_kernel, lats, lons), out_shape=...  16.5 us
    pallas_call x1, Pallas kernels, per_device(): pl.pallas_call(layout_kernel, out_shape=jax.ShapeDtypeStruct(background.s...  1 us

profile of v5, /device:TPU:0, one launch (start us, length us, event | category | flops | bytes accessed | tf_op | source)
XLA Modules:
  0.0 17.5 jit_solution(11674537038632727764)
XLA Ops:
  0.0 16.5 %exchange.1 = (f32[4,768,128]{2,1,0:T(8,128)S(1)}, f32[8,128]{1,0:T(8,128)S(1)}) custom-call(bf16[4,32,2560]{2,1,0:T(8,128)(2,1)} %x_hbm.1, s32[4,64]{1,0:T(4,128)} %col_hbm.1, s32[4,64]{1,0:T(4,128)} %lev_hbm.1, s32[4,64]{1,0:T(4,128)} %mask_hbm.1, f32[4,64]{1,0:T(4,128)} %innov_hbm.1, f32[4,64]{1,0:T(4,128)} %var_hbm.1, s32[4]{0:T(128)} %cols_hbm.1), custom_call_target="tpu_custom_call" | custom-call | tf_op jit(solution)/shard_map/exchange/pallas_call | solution.py:681
  16.5 1.0 %layout.1 = bf16[4,32,2560]{2,1,0:T(8,128)(2,1)} custom-call(f32[4,768,128]{2,1,0:T(8,128)S(1)} %get-tuple-element.7.r_ref, f32[8,128]{1,0:T(8,128)S(1)} %get-tuple-element.8.info_ref), custom_call_target="tpu_custom_call" | custom-call | tf_op jit(solution)/shard_map/layout/pallas_call | solution.py:729

commit v6 on v5

--- a/solution.py
+++ b/solution.py
@@ -16,7 +16,7 @@
 GAP_OWN = 16
 GAP_EARLY = 12
 GAP_LATE = 8
-SHARED = 4
+SHARED = 8
 LANES = 128
 PAIR = 2
 SPAN = GROUP * K

time: 17.7 us -> 17.6 us (level)
  no operation moved by 1% of the time
where the time goes in v6:
time: 17.6 us; the launch traced here: 17.4 us
  Pallas kernels  17.4 us (99%)
    pallas_call x1, Pallas kernels, per_device(): pl.pallas_call(functools.partial(exchange_kernel, lats, lons), out_shape=...  16.4 us
    pallas_call x1, Pallas kernels, per_device(): pl.pallas_call(layout_kernel, out_shape=jax.ShapeDtypeStruct(background.s...  1 us

profile of v6, /device:TPU:0, one launch (start us, length us, event | category | flops | bytes accessed | tf_op | source)
XLA Modules:
  0.0 17.4 jit_solution(10354793297729107810)
XLA Ops:
  0.0 16.4 %exchange.1 = (f32[4,768,128]{2,1,0:T(8,128)S(1)}, f32[8,128]{1,0:T(8,128)S(1)}) custom-call(bf16[4,32,2560]{2,1,0:T(8,128)(2,1)} %x_hbm.1, s32[4,64]{1,0:T(4,128)} %col_hbm.1, s32[4,64]{1,0:T(4,128)} %lev_hbm.1, s32[4,64]{1,0:T(4,128)} %mask_hbm.1, f32[4,64]{1,0:T(4,128)} %innov_hbm.1, f32[4,64]{1,0:T(4,128)} %var_hbm.1, s32[4]{0:T(128)} %cols_hbm.1), custom_call_target="tpu_custom_call" | custom-call | tf_op jit(solution)/shard_map/exchange/pallas_call | solution.py:681
  16.4 1.0 %layout.1 = bf16[4,32,2560]{2,1,0:T(8,128)(2,1)} custom-call(f32[4,768,128]{2,1,0:T(8,128)S(1)} %get-tuple-element.7.r_ref, f32[8,128]{1,0:T(8,128)S(1)} %get-tuple-element.8.info_ref), custom_call_target="tpu_custom_call" | custom-call | tf_op jit(solution)/shard_map/layout/pallas_call | solution.py:729
